TPU v7x, 256 devices: a whole 4x4x8 slice. The times are simulated.
256 devices in a mesh: cond: 2 (over z_hi), gx: 8 (over y, core), yz: 16 (over x, z_lo).
Axes of the slice: x: 4, y: 4, z: 8 (z_hi: 2, z_lo: 4; z = z_hi * 4 + z_lo), core: 2. Of those that a mesh axis runs over, the one named last changes fastest.
Arguments:
- adjoint: float32 [2, 5, 64, 256, 256], P('cond', None, 'gx', 'yz'), may hold values from -6 to 6
- objective_gradient: float32 [2, 5, 64, 256, 256], P('cond', None, 'gx', 'yz'), may hold values from -6 to 6
- diagonal: float32 [64, 256, 256], P('gx', 'yz'), may hold values from 4 to 12
- flux_blocks: float32 [2, 6, 5, 5], P('cond'), may hold values from -1 to 1
- flux_sensitivity: bfloat16 [2, 5, 64, 256, 256], P('cond', None, 'gx', 'yz'), may hold values from -6 to 6
- surface_mask: int32 [64, 256, 256], P('gx', 'yz'), may hold values 0 or 1
- patch_band_slot: int32 [64, 256], P('gx', 'yz'), may hold values from 0 to 62
- design_basis: float32 [256, 128], replicated, may hold values from -0.015625 to 0.015625
- condition_weights: int32 [2], replicated, may hold values from 1 to 999, as said below
Outputs:
- smoothed: float32 [2, 5, 64, 256, 256], P('cond', None, 'gx', 'yz')
- residual: float32 [2, 5, 64, 256, 256], P('cond', None, 'gx', 'yz')
- design_gradient: float32 [4096], P(('gx', 'yz'))
Inputs may be any that keep to these rules, and one draw needn't show every extreme that they name: `condition_weights`: positive integer weights; one condition has weight 999.
All inputs are finite; a program needn't handle non-finite values. No bound on the sum of `surface_mask` on one device may be relied on, other than what follows from the above.
Results may differ from a plain program's by a relative error of at most 0.0003.
Values sent between devices are 32-bit elements; how exact they have to be, the bound alone decides.
A program may use at most 64 MiB of HBM per device.

v0:
```python
import functools

import jax
import jax.numpy as jnp
from jax import lax
from jax.sharding import Mesh
from jax.sharding import PartitionSpec as P

NDES = 4096
GX_YZ = ("gx_0", "gx_1", "yz_0", "yz_1")
GX = ("gx_0", "gx_1")
YZ = ("yz_0", "yz_1")
COND_GX_YZ = ("cond", "gx_0", "gx_1", "yz_0", "yz_1")


relaxation = 0.8
neighbour_starts = ((2, 1, 1), (0, 1, 1), (1, 2, 1), (1, 0, 1), (1, 1, 2), (1, 1, 0))


def padded(x, sides, width):
    edges = {}
    for axis, dim in sides:
        size, length = (lax.axis_size(axis), x.shape[dim])
        up = [(i, (i + 1) % size) for i in range(size - 1)]
        last = lax.slice_in_dim(x, length - width, length, axis=dim)
        initial = lax.slice_in_dim(x, 0, width, axis=dim)
        edges[dim] = (
            lax.ppermute(last, axis, up),
            lax.ppermute(initial, axis, [(b, a) for a, b in up]),
        )
    done = []
    for _, dim in sides:
        low, high = edges[dim]
        around = [(width, width) if d in done else (0, 0) for d in range(x.ndim)]
        x = jnp.concatenate([jnp.pad(low, around), x, jnp.pad(high, around)], axis=dim)
        done.append(dim)
    return x


def one_axis_at_a_time(x, axes):
    return functools.reduce(lax.psum, axes, x)


def apply_operator(padded_field, diagonal, blocks):
    size_x = padded_field.shape[1] - 2
    size_y = padded_field.shape[2] - 2
    size_z = padded_field.shape[3] - 2
    result = diagonal * padded_field[:, 1:-1, 1:-1, 1:-1]
    for direction in range(6):
        start_x, start_y, start_z = neighbour_starts[direction]
        shifted = padded_field[
            :, start_x : start_x + size_x, start_y : start_y + size_y, start_z : start_z + size_z
        ]
        result = result - jnp.einsum(
            "ec,exyz->cxyz", blocks[direction], shifted, precision=lax.Precision.HIGHEST
        )
    return result


def spread_bands(slot_lookup):
    halfway = slot_lookup.shape[1] // 2
    first_half = jnp.pad(slot_lookup[:, :halfway], ((0, 1), (0, 0)))
    second_half = jnp.pad(slot_lookup[:, halfway:], ((1, 0), (0, 0)))
    return (first_half + second_half).reshape(-1)


def pad_third(values):
    return jnp.pad(values, ((0, 0), (0, 0), (0, 0), (1, 1)))


def local(
    adjoint,
    objective_gradient,
    diagonal,
    flux_blocks,
    flux_sensitivity,
    surface_mask,
    patch_band_slot,
    design_basis,
    condition_weights,
):
    blocks = flux_blocks[0]
    source = objective_gradient[0]
    start_field = adjoint[0]

    def operate(values):
        haloed = padded(values, ((GX, 1), (YZ, 2)), 1)
        return apply_operator(pad_third(haloed), diagonal, blocks)

    relaxed = start_field + relaxation * (source - operate(start_field)) / diagonal
    smoothed = relaxed + relaxation * (source - operate(relaxed)) / diagonal
    residual = source - operate(smoothed)
    surface = surface_mask.astype(jnp.float32) * jnp.sum(
        smoothed * flux_sensitivity[0].astype(jnp.float32), axis=0
    )
    projected_gradient = jnp.dot(
        surface.reshape(-1, surface.shape[-1]),
        design_basis,
        precision=lax.Precision.HIGHEST,
        preferred_element_type=jnp.float32,
    )
    slot_count = 2 * NDES // design_basis.shape[1] - 1
    onehot = (jnp.arange(slot_count)[:, None] == patch_band_slot.reshape(1, -1)).astype(jnp.float32)
    slot_lookup = jnp.dot(
        onehot,
        projected_gradient,
        precision=lax.Precision.HIGHEST,
        preferred_element_type=jnp.float32,
    )
    gradient = spread_bands(slot_lookup)
    weights_float = condition_weights.astype(jnp.float32)
    picked = jnp.arange(weights_float.shape[0]) == lax.axis_index("cond")
    local_portion = jnp.sum(jnp.where(picked, weights_float, 0.0)) / jnp.sum(weights_float)
    summed = one_axis_at_a_time(local_portion * gradient, COND_GX_YZ)
    pieces = NDES // lax.axis_size(GX_YZ)
    design_gradient = lax.dynamic_slice_in_dim(summed, lax.axis_index(GX_YZ) * pieces, pieces, 0)
    return (smoothed[None], residual[None], design_gradient)


def solution(mesh):
    torus = Mesh(
        mesh.devices.reshape(mesh.shape["cond"], 4, 2, 4, 4),
        ("cond", "gx_0", "gx_1", "yz_0", "yz_1"),
    )
    in_specs = (
        P("cond", None, GX, YZ, None),
        P("cond", None, GX, YZ, None),
        P(GX, YZ, None),
        P("cond", None, None, None),
        P("cond", None, GX, YZ, None),
        P(GX, YZ, None),
        P(GX, YZ),
        P(),
        P(),
    )
    out_specs = (P("cond", None, GX, YZ, None), P("cond", None, GX, YZ, None), P(GX_YZ))
    return jax.shard_map(local, mesh=torus, in_specs=in_specs, out_specs=out_specs, check_vma=False)
```

profile of v0, /device:TPU:0, one launch (start us, length us, event | category | flops | bytes accessed | tf_op | source)
XLA Modules:
  0.0 146.4 jit_solution(6187131229460594439)
XLA Ops:
  0.7 1.5 %copy.88 = f32[1,5,8,16,256]{4,1,3,2,0:T(8,128)S(1)} copy(f32[1,5,8,16,256]{4,3,2,1,0:T(8,128)} %param.9) | data formatting | bytes 1310720 | tf_op args[0]
  2.2 1.3 collective-permute-start.2
  3.5 4.5 %collective-permute-start.3 = (f32[5,8,1,256]{3,0,2,1:T(8,128)S(1)}, f32[5,8,1,256]{3,0,2,1:T(8,128)S(1)}, u32[]{:S(2)}, u32[]{:S(2)}) collective-permute-start(f32[5,8,1,256]{3,0,2,1:T(8,128)S(1)} %get-tuple-element.18), channel_id=1, source_target_pairs={{0,1},{1,2},{2,3},{3,4},{4,5},{5,6},{6,7},{7,8},{8,9},{9,10},{10,1... | collective-permute-start | bytes 122888 | tf_op jit(solution)/shard_map/ppermute | solution.py:28
  8.1 1.3 collective-permute-start
  9.4 3.0 %collective-permute-start.1 = (f32[5,1,16,256]{3,0,2,1:T(8,128)S(1)}, f32[5,1,16,256]{3,0,2,1:T(8,128)S(1)}, u32[]{:S(2)}, u32[]{:S(2)}) collective-permute-start(f32[5,1,16,256]{3,0,2,1:T(8,128)S(1)} %get-tuple-element.16), channel_id=1, source_target_pairs={{0,16},{16,32},{32,48},{48,64},{64,80},{80,96},{96,112},{1,17},{17... | collective-permute-start | bytes 245768 | tf_op jit(solution)/shard_map/ppermute | solution.py:28
  15.2 1.2 convolution_bitcast_fusion.11
  16.5 1.1 fusion.61
  17.6 1.1 fusion.64
  18.6 1.1 convolution_bitcast_fusion.4
  19.8 2.0 %fusion.94 = f32[5,8,16,256]{3,0,2,1:T(8,128)S(1)} fusion(f32[5,8,16,256]{3,0,2,1:T(8,128)S(1)} %bitcast.184, f32[5,8,16,256]{3,0,2,1:T(8,128)S(1)} %convolution_bitcast_fusion.10, f32[5,8,16,256]{3,0,2,1:T(8,128)S(1)} %convolution_bitcast_fusion.11, f32[5,8,16,256]{3,0,2,1:T(8,128)S(1)} %fusion.61, f32[5,8,16,256]{3,0,2,1:T(8,128)S(1)} %fusion.64, ...), kind=kOutput, calls=%fused_computation.108 | convolution fusion | flops 11816960 | bytes 5455972 | tf_op jit(solution)/shard_map/ec,exyz->cxyz/dot_general | solution.py:54
  21.8 1.3 collective-permute-start.6
  23.1 4.5 %collective-permute-start.7 = (f32[5,8,1,256]{3,0,2,1:T(8,128)S(1)}, f32[5,8,1,256]{3,0,2,1:T(8,128)S(1)}, u32[]{:S(2)}, u32[]{:S(2)}) collective-permute-start(f32[5,8,1,256]{3,0,2,1:T(8,128)S(1)} %get-tuple-element.14), channel_id=1, source_target_pairs={{0,1},{1,2},{2,3},{3,4},{4,5},{5,6},{6,7},{7,8},{8,9},{9,10},{10,1... | collective-permute-start | bytes 122888 | tf_op jit(solution)/shard_map/ppermute | solution.py:28
  27.7 1.3 collective-permute-start.4
  29.0 3.2 %collective-permute-start.5 = (f32[5,1,16,256]{3,0,2,1:T(8,128)S(1)}, f32[5,1,16,256]{3,0,2,1:T(8,128)S(1)}, u32[]{:S(2)}, u32[]{:S(2)}) collective-permute-start(f32[5,1,16,256]{3,0,2,1:T(8,128)S(1)} %get-tuple-element.12), channel_id=1, source_target_pairs={{0,16},{16,32},{32,48},{48,64},{64,80},{80,96},{96,112},{1,17},{17... | collective-permute-start | bytes 245768 | tf_op jit(solution)/shard_map/ppermute | solution.py:28
  36.0 1.2 convolution_bitcast_fusion.9
  37.2 1.1 fusion.55
  38.3 1.1 fusion.58
  39.4 1.1 convolution_bitcast_fusion.2
  40.5 2.2 %fusion.119 = (f32[8,16,256]{2,1,0:T(8,128)S(1)}, f32[5,8,16,256]{3,0,2,1:T(8,128)S(1)}) fusion(bf16[1,5,8,16,256]{4,3,2,1,0:T(8,128)(2,1)S(1)} %copy-done.3, f32[5,8,16,256]{3,0,2,1:T(8,128)S(1)} %fusion.94, f32[5,8,16,256]{3,0,2,1:T(8,128)S(1)} %convolution_bitcast_fusion.8, f32[5,8,16,256]{3,0,2,1:T(8,128)S(1)} %convolution_bitcast_fusion.9, ...), kind=kOutput, calls=%fused_computation.134 | convolution fusion | flops 12275712 | bytes 5914724 | tf_op jit(solution)/shard_map/ec,exyz->cxyz/dot_general | solution.py:54
  42.7 1.3 collective-permute-start.10
  44.0 4.5 %collective-permute-start.11 = (f32[5,8,1,256]{3,0,2,1:T(8,128)S(1)}, f32[5,8,1,256]{3,0,2,1:T(8,128)S(1)}, u32[]{:S(2)}, u32[]{:S(2)}) collective-permute-start(f32[5,8,1,256]{3,0,2,1:T(8,128)S(1)} %get-tuple-element.10), channel_id=1, source_target_pairs={{0,1},{1,2},{2,3},{3,4},{4,5},{5,6},{6,7},{7,8},{8,9},{9,10},{10,1... | collective-permute-start | bytes 122888 | tf_op jit(solution)/shard_map/ppermute | solution.py:28
  48.6 1.3 collective-permute-start.8
  49.9 4.8 %collective-permute-start.9 = (f32[5,1,16,256]{3,0,2,1:T(8,128)S(1)}, f32[5,1,16,256]{3,0,2,1:T(8,128)S(1)}, u32[]{:S(2)}, u32[]{:S(2)}) collective-permute-start(f32[5,1,16,256]{3,0,2,1:T(8,128)S(1)} %get-tuple-element.8), channel_id=1, source_target_pairs={{0,16},{16,32},{32,48},{48,64},{64,80},{80,96},{96,112},{1,17},{17... | collective-permute-start | bytes 245768 | tf_op jit(solution)/shard_map/ppermute | solution.py:28
  55.3 17.2 %psum.35 = f32[4096]{0:T(1024)S(1)} all-reduce(f32[4096]{0:T(1024)S(1)} %mul.63), channel_id=1, replica_groups=mesh['cond'=2,'gx_0'=4,'gx_1'=2,'yz_0'=4,'yz_1'=4] {'cond'}, use_global_device_ids=true, to_apply=%region_3.4 | all-reduce | flops 4096 | bytes 32768 | tf_op jit(solution)/shard_map/psum | solution.py:41
  72.5 18.6 %psum.36 = f32[4096]{0:T(1024)S(1)} all-reduce(f32[4096]{0:T(1024)S(1)} %psum.35), channel_id=1, replica_groups=mesh['cond'=2,'gx_0'=4,'gx_1'=2,'yz_0'=4,'yz_1'=4] {'gx_0'}, use_global_device_ids=true, to_apply=%region_4.5 | all-reduce | flops 4096 | bytes 32768 | tf_op jit(solution)/shard_map/psum | solution.py:41
  91.1 3.3 %psum.37 = f32[4096]{0:T(1024)S(1)} all-reduce(f32[4096]{0:T(1024)S(1)} %psum.36), channel_id=1, replica_groups=mesh['cond'=2,'gx_0'=4,'gx_1'=2,'yz_0'=4,'yz_1'=4] {'gx_1'}, use_global_device_ids=true, to_apply=%region_5.6 | all-reduce | flops 4096 | bytes 32768 | tf_op jit(solution)/shard_map/psum | solution.py:41
  95.5 22.5 %psum.38 = f32[4096]{0:T(1024)S(1)} all-reduce(f32[4096]{0:T(1024)S(1)} %psum.37), channel_id=1, replica_groups=mesh['cond'=2,'gx_0'=4,'gx_1'=2,'yz_0'=4,'yz_1'=4] {'yz_0'}, use_global_device_ids=true, to_apply=%region_6.7 | all-reduce | flops 4096 | bytes 32768 | tf_op jit(solution)/shard_map/psum | solution.py:41
  118.0 18.6 %psum.39 = f32[4096]{0:T(1024)S(1)} all-reduce(f32[4096]{0:T(1024)S(1)} %psum.38), channel_id=1, replica_groups=mesh['cond'=2,'gx_0'=4,'gx_1'=2,'yz_0'=4,'yz_1'=4] {'yz_1'}, use_global_device_ids=true, to_apply=%region_7.8 | all-reduce | flops 4096 | bytes 32768 | tf_op jit(solution)/shard_map/psum | solution.py:41
  138.9 1.2 convolution_bitcast_fusion.7
  141.2 1.1 fusion.52
  142.3 1.1 convolution_bitcast_fusion
  143.3 2.0 %fusion.86 = f32[1,5,8,16,256]{4,1,3,2,0:T(8,128)S(1)} fusion(f32[5,8,16,256]{3,0,2,1:T(8,128)S(1)} %convolution_bitcast_fusion.6, f32[5,8,16,256]{3,0,2,1:T(8,128)S(1)} %convolution_bitcast_fusion.7, f32[5,8,16,256]{3,0,2,1:T(8,128)S(1)} %fusion.49, f32[5,8,16,256]{3,0,2,1:T(8,128)S(1)} %fusion.52, f32[5,8,16,256]{3,0,2,1:T(8,128)S(1)} %convolution_bitcast_fusion, ...), kind=kOutput, calls=%fused_computation.100 | convolution fusion | flops 11325440 | bytes 5455972 | tf_op jit(solution)/shard_map/ec,exyz->cxyz/dot_general | solution.py:54
  (65 shorter events, 11.3 us)
Async XLA Ops:
  0.6 54.1 %copy-start = (f32[256,128]{1,0:T(8,128)S(1)}, f32[256,128]{1,0:T(8,128)}, u32[]{:S(2)}) copy-start(f32[256,128]{1,0:T(8,128)} %param.16) | copy-start | bytes 393220
  0.6 11.8 %copy-start.4 = (f32[1,6,5,5]{1,0,3,2:T(1,128)S(1)}, f32[1,6,5,5]{1,0,3,2:T(1,128)}, u32[]{:S(2)}) copy-start(f32[1,6,5,5]{1,0,3,2:T(1,128)} %param.12) | copy-start | bytes 1804
  2.2 11.2 %collective-permute-start.2 = (f32[5,8,1,256]{3,0,2,1:T(8,128)S(1)}, f32[5,8,1,256]{3,0,2,1:T(8,128)S(1)}, u32[]{:S(2)}, u32[]{:S(2)}) collective-permute-start(f32[5,8,1,256]{3,0,2,1:T(8,128)S(1)} %get-tuple-element.19), channel_id=1, source_target_pairs={{1,0},{2,1},{3,2},{4,3},{5,4},{6,5},{7,6},{8,7},{9,8},{10,9},{11,1... | collective-permute-start | bytes 122888 | tf_op jit(solution)/shard_map/ppermute | solution.py:29
  3.5 10.0 %collective-permute-start.3 = (f32[5,8,1,256]{3,0,2,1:T(8,128)S(1)}, f32[5,8,1,256]{3,0,2,1:T(8,128)S(1)}, u32[]{:S(2)}, u32[]{:S(2)}) collective-permute-start(f32[5,8,1,256]{3,0,2,1:T(8,128)S(1)} %get-tuple-element.18), channel_id=1, source_target_pairs={{0,1},{1,2},{2,3},{3,4},{4,5},{5,6},{6,7},{7,8},{8,9},{9,10},{10,1... | collective-permute-start | bytes 122888 | tf_op jit(solution)/shard_map/ppermute | solution.py:28
  8.1 5.4 %collective-permute-start = (f32[5,1,16,256]{3,0,2,1:T(8,128)S(1)}, f32[5,1,16,256]{3,0,2,1:T(8,128)S(1)}, u32[]{:S(2)}, u32[]{:S(2)}) collective-permute-start(f32[5,1,16,256]{3,0,2,1:T(8,128)S(1)} %get-tuple-element.17), channel_id=1, source_target_pairs={{16,0},{32,16},{48,32},{64,48},{80,64},{96,80},{112,96},{17,1},{33... | collective-permute-start | bytes 245768 | tf_op jit(solution)/shard_map/ppermute | solution.py:29
  9.4 4.1 %collective-permute-start.1 = (f32[5,1,16,256]{3,0,2,1:T(8,128)S(1)}, f32[5,1,16,256]{3,0,2,1:T(8,128)S(1)}, u32[]{:S(2)}, u32[]{:S(2)}) collective-permute-start(f32[5,1,16,256]{3,0,2,1:T(8,128)S(1)} %get-tuple-element.16), channel_id=1, source_target_pairs={{0,16},{16,32},{32,48},{48,64},{64,80},{80,96},{96,112},{1,17},{17... | collective-permute-start | bytes 245768 | tf_op jit(solution)/shard_map/ppermute | solution.py:28
  17.5 2.2 %copy-start.1 = (f32[1,5,8,16,256]{4,3,2,1,0:T(8,128)S(1)}, f32[1,5,8,16,256]{4,3,2,1,0:T(8,128)}, u32[]{:S(2)}) copy-start(f32[1,5,8,16,256]{4,3,2,1,0:T(8,128)} %param.10) | copy-start | bytes 1966084
  17.5 2.2 %copy-start.2 = (f32[8,16,256]{2,1,0:T(8,128)S(1)}, f32[8,16,256]{2,1,0:T(8,128)}, u32[]{:S(2)}) copy-start(f32[8,16,256]{2,1,0:T(8,128)} %param.11) | copy-start | bytes 393220
  19.7 12.5 %copy-start.7 = (s32[2]{0:T(128)S(1)}, s32[2]{0:T(128)}, u32[]{:S(2)}) copy-start(s32[2]{0:T(128)} %param.17) | copy-start | bytes 28
  19.7 13.1 %copy-start.6 = (s32[8,16]{1,0:T(8,128)S(1)}, s32[8,16]{1,0:T(8,128)}, u32[]{:S(2)}) copy-start(s32[8,16]{1,0:T(8,128)} %param.15) | copy-start | bytes 1540
  21.8 12.4 %collective-permute-start.6 = (f32[5,8,1,256]{3,0,2,1:T(8,128)S(1)}, f32[5,8,1,256]{3,0,2,1:T(8,128)S(1)}, u32[]{:S(2)}, u32[]{:S(2)}) collective-permute-start(f32[5,8,1,256]{3,0,2,1:T(8,128)S(1)} %get-tuple-element.15), channel_id=1, source_target_pairs={{1,0},{2,1},{3,2},{4,3},{5,4},{6,5},{7,6},{8,7},{9,8},{10,9},{11,1... | collective-permute-start | bytes 122888 | tf_op jit(solution)/shard_map/ppermute | solution.py:29
  23.1 11.2 %collective-permute-start.7 = (f32[5,8,1,256]{3,0,2,1:T(8,128)S(1)}, f32[5,8,1,256]{3,0,2,1:T(8,128)S(1)}, u32[]{:S(2)}, u32[]{:S(2)}) collective-permute-start(f32[5,8,1,256]{3,0,2,1:T(8,128)S(1)} %get-tuple-element.14), channel_id=1, source_target_pairs={{0,1},{1,2},{2,3},{3,4},{4,5},{5,6},{6,7},{7,8},{8,9},{9,10},{10,1... | collective-permute-start | bytes 122888 | tf_op jit(solution)/shard_map/ppermute | solution.py:28
  27.7 6.6 %collective-permute-start.4 = (f32[5,1,16,256]{3,0,2,1:T(8,128)S(1)}, f32[5,1,16,256]{3,0,2,1:T(8,128)S(1)}, u32[]{:S(2)}, u32[]{:S(2)}) collective-permute-start(f32[5,1,16,256]{3,0,2,1:T(8,128)S(1)} %get-tuple-element.13), channel_id=1, source_target_pairs={{16,0},{32,16},{48,32},{64,48},{80,64},{96,80},{112,96},{17,1},{33... | collective-permute-start | bytes 245768 | tf_op jit(solution)/shard_map/ppermute | solution.py:29
  29.0 5.3 %collective-permute-start.5 = (f32[5,1,16,256]{3,0,2,1:T(8,128)S(1)}, f32[5,1,16,256]{3,0,2,1:T(8,128)S(1)}, u32[]{:S(2)}, u32[]{:S(2)}) collective-permute-start(f32[5,1,16,256]{3,0,2,1:T(8,128)S(1)} %get-tuple-element.12), channel_id=1, source_target_pairs={{0,16},{16,32},{32,48},{48,64},{64,80},{80,96},{96,112},{1,17},{17... | collective-permute-start | bytes 245768 | tf_op jit(solution)/shard_map/ppermute | solution.py:28
  38.3 2.2 %copy-start.3 = (bf16[1,5,8,16,256]{4,3,2,1,0:T(8,128)(2,1)S(1)}, bf16[1,5,8,16,256]{4,3,2,1,0:T(8,128)(2,1)}, u32[]{:S(2)}) copy-start(bf16[1,5,8,16,256]{4,3,2,1,0:T(8,128)(2,1)} %param.13) | copy-start | bytes 983044
  40.5 14.2 %copy-start.5 = (s32[8,16,256]{2,1,0:T(8,128)S(1)}, s32[8,16,256]{2,1,0:T(8,128)}, u32[]{:S(2)}) copy-start(s32[8,16,256]{2,1,0:T(8,128)} %param.14) | copy-start | bytes 393220
  42.7 94.4 %collective-permute-start.10 = (f32[5,8,1,256]{3,0,2,1:T(8,128)S(1)}, f32[5,8,1,256]{3,0,2,1:T(8,128)S(1)}, u32[]{:S(2)}, u32[]{:S(2)}) collective-permute-start(f32[5,8,1,256]{3,0,2,1:T(8,128)S(1)} %get-tuple-element.11), channel_id=1, source_target_pairs={{1,0},{2,1},{3,2},{4,3},{5,4},{6,5},{7,6},{8,7},{9,8},{10,9},{11,1... | collective-permute-start | bytes 122888 | tf_op jit(solution)/shard_map/ppermute | solution.py:29
  44.0 93.1 %collective-permute-start.11 = (f32[5,8,1,256]{3,0,2,1:T(8,128)S(1)}, f32[5,8,1,256]{3,0,2,1:T(8,128)S(1)}, u32[]{:S(2)}, u32[]{:S(2)}) collective-permute-start(f32[5,8,1,256]{3,0,2,1:T(8,128)S(1)} %get-tuple-element.10), channel_id=1, source_target_pairs={{0,1},{1,2},{2,3},{3,4},{4,5},{5,6},{6,7},{7,8},{8,9},{9,10},{10,1... | collective-permute-start | bytes 122888 | tf_op jit(solution)/shard_map/ppermute | solution.py:28
  48.6 88.6 %collective-permute-start.8 = (f32[5,1,16,256]{3,0,2,1:T(8,128)S(1)}, f32[5,1,16,256]{3,0,2,1:T(8,128)S(1)}, u32[]{:S(2)}, u32[]{:S(2)}) collective-permute-start(f32[5,1,16,256]{3,0,2,1:T(8,128)S(1)} %get-tuple-element.9), channel_id=1, source_target_pairs={{16,0},{32,16},{48,32},{64,48},{80,64},{96,80},{112,96},{17,1},{33... | collective-permute-start | bytes 245768 | tf_op jit(solution)/shard_map/ppermute | solution.py:29
  49.9 87.3 %collective-permute-start.9 = (f32[5,1,16,256]{3,0,2,1:T(8,128)S(1)}, f32[5,1,16,256]{3,0,2,1:T(8,128)S(1)}, u32[]{:S(2)}, u32[]{:S(2)}) collective-permute-start(f32[5,1,16,256]{3,0,2,1:T(8,128)S(1)} %get-tuple-element.8), channel_id=1, source_target_pairs={{0,16},{16,32},{32,48},{48,64},{64,80},{80,96},{96,112},{1,17},{17... | collective-permute-start | bytes 245768 | tf_op jit(solution)/shard_map/ppermute | solution.py:28
where the time goes:
time: 147 us; the launch traced here: 146 us
  blocking collectives  80.2 us (55%)
  starting transfers between devices  32.4 us (22%)
  matrix products  23 us (16%)
  local copies, waits for them, and re-layouts  5.6 us (4%)
  other arithmetic  2.59 us (2%)
  between operations  2.56 us (2%)
    psum x5, blocking collectives, one_axis_at_a_time(): return functools.reduce(lax.psum, axes, x)  80.2 us
    ppermute x6, starting transfers between devices, padded(): lax.ppermute(last, axis, up)  24.7 us
    dot_general x18, matrix products, apply_operator(): jnp.einsum('ec,exyz->cxyz', blocks[direction], shifted, precision=lax.Pre...  22.6 us
    ppermute x6, starting transfers between devices, padded(): lax.ppermute(initial, axis, [(b, a) for a, b in up])  7.75 us
    unnamed x25, local copies, waits for them, and re-layouts  4.44 us
  transfers between devices with their start and end apart: 12, of which 0 were waited for; matrix products, arithmetic and copies ran while one was open for 3% of the time, Pallas kernels for 0%

commit v1 on v0

v1 whole, which is shorter than its diff:
```python
import functools

import jax
import jax.numpy as jnp
from jax import lax
from jax.experimental import pallas as pl
from jax.experimental.pallas import tpu as pltpu
from jax.sharding import Mesh
from jax.sharding import PartitionSpec as P

NDES = 4096
NVAR = 5
LANES = 128
SUBLANES = 8
AXES = ("cond", "gx_0", "gx_1", "yz_0", "yz_1")
GX = ("gx_0", "gx_1")
YZ = ("yz_0", "yz_1")
GX_YZ = GX + YZ
MESH = pl.DeviceIdType.MESH
RELAX = 0.8
X_HI, X_LO, Y_HI, Y_LO, Z_HI, Z_LO = range(6)


def kernel(
    dims,
    adjoint,
    objective,
    diagonal,
    sensitivity,
    mask,
    basis,
    blocks,
    weights,
    slots,
    smoothed,
    residual,
    gradient,
    start,
    relaxed,
    source,
    diag,
    ratio,
    sens,
    surface_mask,
    base,
    surface,
    onehot,
    halo_x,
    halo_y,
    face_y,
    outgoing,
    plane_in,
    row_out,
    column_in,
    local_sem,
    halo_send,
    halo_recv,
    plane_send,
    plane_recv,
    column_send,
    column_recv,
):
    n_cond, n_y, n_core, n_x, n_zl = dims
    nx, ny = slots.shape
    rows = nx * ny
    n_row, n_col = ny // SUBLANES, basis.shape[0] // LANES
    span = n_row * n_col * SUBLANES
    n_gx, n_yz, n_plane, n_z = n_y * n_core, n_x * n_zl, n_y * n_core * n_x, n_cond * n_zl

    cond, y, core, x, zl = (lax.axis_index(a) for a in AXES)
    gx, yz = y * n_core + core, x * n_zl + zl
    plane, z = gx * n_x + x, cond * n_zl + zl

    def at_gx(g):
        return (cond, g // n_core, g % n_core, x, zl)

    def at_yz(q):
        return (cond, y, core, q // n_zl, q % n_zl)

    def at_plane(p):
        g = p // n_x
        return (cond, g // n_core, g % n_core, p % n_x, zl)

    def at_z(q):
        return (q // n_zl, y, core, x, q % n_zl)

    pairs = (
        (adjoint, start),
        (diagonal, diag),
        (objective, source),
        (mask, surface_mask),
        (sensitivity, sens),
        (basis, base),
    )
    loads = [pltpu.make_async_copy(a, b, local_sem.at[i]) for i, (a, b) in enumerate(pairs)]
    load_start, load_diag, load_source, load_mask, load_sens, load_base = loads
    for load in loads:
        load.start()

    barrier = pltpu.get_barrier_semaphore()

    def greet(target):
        pl.semaphore_signal(barrier, inc=1, device_id=target, device_id_type=MESH)

    step_up = jnp.logical_and(zl == n_zl - 1, x < n_x - 1)
    step_down = jnp.logical_and(zl == 0, x > 0)

    @pl.when(step_up)
    def _():
        greet(at_yz(yz + 1))

    @pl.when(step_down)
    def _():
        greet(at_yz(yz - 1))

    for o in range(1, n_z):
        greet(at_z((z + o) % n_z))
    for o in range(1, n_plane):
        greet(at_plane((plane + o) % n_plane))

    sides = (
        (gx > 0, gx < n_gx - 1),
        (yz > 0, yz < n_yz - 1),
    )

    for axis, buffer in ((0, halo_x), (1, halo_y)):
        for side in range(2):

            @pl.when(jnp.logical_not(sides[axis][side]))
            def _(buffer=buffer, side=side):
                buffer[:, side] = jnp.zeros_like(buffer[:, side])

    def halo_copy(field, turn, axis, side):
        index = 2 * axis + side
        if axis == 0:
            src = field.at[:, pl.ds((nx - 1) * span if side else 0, span)]
            dst = halo_x.at[turn, 1 - side]
            target = at_gx(gx + 1 if side else gx - 1)
        else:
            src = face_y.at[turn, side]
            dst = halo_y.at[turn, 1 - side]
            target = at_yz(yz + 1 if side else yz - 1)
        return pltpu.make_async_remote_copy(
            src_ref=src,
            dst_ref=dst,
            send_sem=halo_send.at[turn, index],
            recv_sem=halo_recv.at[turn, 2 * axis + 1 - side],
            device_id=target,
            device_id_type=MESH,
        )

    def each_side(body):
        for axis in (1, 0):
            for side in range(2):

                @pl.when(sides[axis][side])
                def _(axis=axis, side=side):
                    body(axis, side)

    def line(side, c):
        first = ((n_row - 1) * n_col + c) * SUBLANES + SUBLANES - 1 if side else c * SUBLANES
        return pl.ds(first, nx, stride=span)

    def pack_faces(field, turn):
        for side in range(2):
            for e in range(NVAR):
                for c in range(n_col):
                    face_y[turn, side, e, pl.ds(c * nx, nx), :] = field[e, line(side, c), :]

    def send_faces(field, turn):
        each_side(lambda axis, side: halo_copy(field, turn, axis, side).start())

    def wait_faces(turn):
        def body(axis, side):
            pltpu.make_async_remote_copy(
                src_ref=(halo_x if axis == 0 else halo_y).at[turn, side],
                dst_ref=(halo_x if axis == 0 else halo_y).at[turn, side],
                send_sem=halo_send.at[turn, 2 * axis + side],
                recv_sem=halo_recv.at[turn, 2 * axis + side],
                device_id=at_gx(gx) if axis == 0 else at_yz(yz),
                device_id_type=MESH,
            ).wait_recv()

        each_side(body)

    def drain_faces(field, turn):
        each_side(lambda axis, side: halo_copy(field, turn, axis, side).wait_send())

    tiles = [(r, c) for r in range(n_row) for c in range(n_col)]

    def window(block, r, c):
        at = block * span + (r * n_col + c) * SUBLANES
        return pl.ds(at if isinstance(at, int) else pl.multiple_of(at, SUBLANES), SUBLANES)

    def neighbours(field, block, lo, hi):
        sub = lax.broadcasted_iota(jnp.int32, (SUBLANES, LANES), 0)
        lane = lax.broadcasted_iota(jnp.int32, (SUBLANES, LANES), 1)
        zero = jnp.zeros((SUBLANES, LANES), jnp.float32)

        def tile_of(e, b, r, c):
            return field[e, window(b, r, c), :]

        total = [[None] * len(tiles) for _ in range(NVAR)]
        for e in range(NVAR):
            here = {rc: tile_of(e, block, *rc) for rc in tiles}
            terms = {}
            if hi:
                terms[X_HI] = {rc: tile_of(e, block + 1, *rc) for rc in tiles}
            if lo:
                terms[X_LO] = {rc: tile_of(e, block - 1, *rc) for rc in tiles}
            for d, shift, axis, index, edge in (
                (Y_HI, SUBLANES - 1, 0, sub, SUBLANES - 1),
                (Y_LO, 1, 0, sub, 0),
                (Z_HI, LANES - 1, 1, lane, LANES - 1),
                (Z_LO, 1, 1, lane, 0),
            ):
                turned = {rc: pltpu.roll(here[rc], shift, axis) for rc in tiles}
                step = 1 if edge else -1
                moved = {}
                for r, c in tiles:
                    beside = (r + step, c) if axis == 0 else (r, c + step)
                    moved[r, c] = jnp.where(index == edge, turned.get(beside, zero), turned[r, c])
                terms[d] = moved
            for d, values in terms.items():
                for k in range(NVAR):
                    coef = blocks[0, d, e, k]
                    for i, rc in enumerate(tiles):
                        part = coef * values[rc]
                        total[k][i] = part if total[k][i] is None else total[k][i] + part
        return total

    def over_blocks(body):
        body(0, False, True)

        def inner(b, carry):
            body(b, True, True)
            return carry

        lax.fori_loop(1, nx - 1, inner, 0)
        body(nx - 1, True, False)

    def sweep(field, result):
        def body(block, lo, hi):
            total = neighbours(field, block, lo, hi)
            for i, rc in enumerate(tiles):
                at = window(block, *rc)
                scale = ratio[at, :]
                for k in range(NVAR):
                    result[k, at, :] = (1.0 - RELAX) * field[k, at, :] + scale * (
                        source[k, at, :] + total[k][i]
                    )

        over_blocks(body)

    def operate(field, result):
        def body(block, lo, hi):
            total = neighbours(field, block, lo, hi)
            for i, rc in enumerate(tiles):
                at = window(block, *rc)
                scale = diag[at, :]
                for k in range(NVAR):
                    result[k, at, :] = source[k, at, :] - scale * field[k, at, :] + total[k][i]

        over_blocks(body)

    def add_halos(turn, result, scale):
        for axis, buffer in ((0, halo_x), (1, halo_y)):
            for side in range(2):
                d = (X_LO, X_HI, Y_LO, Y_HI)[2 * axis + side]
                if axis == 0:
                    first = (nx - 1) * span if side else 0
                    parts = [(pl.ds(first + i, SUBLANES), pl.ds(i, SUBLANES)) for i in range(0, span, SUBLANES)]
                else:
                    parts = [(line(side, c), pl.ds(c * nx, nx)) for c in range(n_col)]
                for at, place in parts:
                    factor = None if scale is None else scale[at, :]
                    outside = [buffer[turn, side, e, place, :] for e in range(NVAR)]
                    for k in range(NVAR):
                        part = blocks[0, d, 0, k] * outside[0]
                        for e in range(1, NVAR):
                            part = part + blocks[0, d, e, k] * outside[e]
                        part = part if factor is None else factor * part
                        result[k, at, :] = result[k, at, :] + part

    load_start.wait()
    pack_faces(start, 0)
    pl.semaphore_wait(
        barrier, n_z + n_plane - 2 + step_up.astype(jnp.int32) + step_down.astype(jnp.int32)
    )
    send_faces(start, 0)

    load_diag.wait()
    ratio[...] = RELAX / diag[...]
    load_source.wait()
    sweep(start, relaxed)

    pick = lax.broadcasted_iota(jnp.int32, (ny, rows), 1) % ny == lax.broadcasted_iota(jnp.int32, (ny, rows), 0)
    spread = jnp.dot(
        slots[...].astype(jnp.float32), pick.astype(jnp.float32), preferred_element_type=jnp.float32
    )
    own = lax.broadcasted_iota(jnp.int32, (nx, rows), 1) // ny == lax.broadcasted_iota(jnp.int32, (nx, rows), 0)
    slot_row = jnp.sum(jnp.where(own, spread, 0.0), axis=0, keepdims=True)
    n_out = NDES // LANES
    number = lax.broadcasted_iota(jnp.int32, (3 * n_out, rows), 0)
    third = number // n_out
    wanted = 2 * (number % n_out) + jnp.where(third == 0, 0, jnp.where(third == 1, -1, 1))
    onehot[...] = jnp.where(slot_row == wanted.astype(jnp.float32), 1.0, 0.0)

    wait_faces(0)
    add_halos(0, relaxed, ratio)
    pack_faces(relaxed, 1)
    send_faces(relaxed, 1)
    sweep(relaxed, smoothed)
    load_mask.wait()
    load_sens.wait()
    load_base.wait()
    drain_faces(start, 0)

    wait_faces(1)
    add_halos(1, smoothed, ratio)
    pack_faces(smoothed, 2)
    send_faces(smoothed, 2)

    for block in range(nx):
        for c in range(n_col):
            cols = pl.ds(c * LANES, LANES)
            weight = [sens[k, pl.ds(block * ny, ny), cols].astype(jnp.float32) for k in range(NVAR)]
            for r in range(n_row):
                at = window(block, r, c)
                part = [
                    smoothed[k, at, :] * weight[k][r * SUBLANES : (r + 1) * SUBLANES] for k in range(NVAR)
                ]
                surface[pl.ds(block * ny + r * SUBLANES, SUBLANES), cols] = surface_mask[at, :].astype(
                    jnp.float32
                ) * functools.reduce(jnp.add, part)
    projected = jnp.dot(
        surface[...], base[...], precision=lax.Precision.HIGHEST, preferred_element_type=jnp.float32
    )
    looked = jnp.dot(
        onehot[...], projected, precision=lax.Precision.HIGHEST, preferred_element_type=jnp.float32
    )
    even, before, after = (looked[i * n_out : (i + 1) * n_out] for i in range(3))
    half = lax.broadcasted_iota(jnp.int32, (n_out, LANES), 1) < LANES // 2
    swapped = pltpu.roll(jnp.where(half, after, before), LANES // 2, 1)
    whole = jnp.full((n_out, LANES), (weights[0] + weights[1]).astype(jnp.float32))
    mine = jnp.where(cond == 0, weights[0], weights[1]).astype(jnp.float32)
    scaled = (even + swapped) * (jnp.full((n_out, LANES), mine) / whole)
    outgoing[...] = scaled.reshape(n_out, 1, LANES)

    def plane_copy(o):
        target = (plane + o) % n_plane
        return pltpu.make_async_remote_copy(
            src_ref=outgoing.at[target],
            dst_ref=plane_in.at[plane],
            send_sem=plane_send,
            recv_sem=plane_recv,
            device_id=at_plane(target),
            device_id_type=MESH,
        )

    for o in range(1, n_plane):
        plane_copy(o).start()
    plane_in[plane] = outgoing[plane]

    operate(smoothed, residual)
    drain_faces(relaxed, 1)

    everyone = pltpu.make_async_remote_copy(
        src_ref=outgoing.at[pl.ds(0, n_plane - 1)],
        dst_ref=plane_in.at[pl.ds(0, n_plane - 1)],
        send_sem=plane_send,
        recv_sem=plane_recv,
        device_id=at_plane(plane),
        device_id_type=MESH,
    )
    everyone.wait_recv()
    row = plane_in[0]
    for i in range(1, n_plane):
        row = row + plane_in[i]
    row_out[0] = row
    column_in[z] = row

    def column_copy(o):
        return pltpu.make_async_remote_copy(
            src_ref=row_out.at[0],
            dst_ref=column_in.at[z],
            send_sem=column_send.at[o - 1],
            recv_sem=column_recv,
            device_id=at_z((z + o) % n_z),
            device_id_type=MESH,
        )

    for o in range(1, n_z):
        column_copy(o).start()

    wait_faces(2)
    add_halos(2, residual, None)
    everyone.wait_send()
    drain_faces(smoothed, 2)

    pltpu.make_async_remote_copy(
        src_ref=column_in.at[pl.ds(0, n_z - 1)],
        dst_ref=column_in.at[pl.ds(0, n_z - 1)],
        send_sem=column_send.at[0],
        recv_sem=column_recv,
        device_id=at_z(z),
        device_id_type=MESH,
    ).wait_recv()
    row = column_in[0]
    for i in range(1, n_z):
        row = row + column_in[i]
    width = LANES // n_zl
    part = row[:, :width]
    for q in range(1, n_zl):
        part = jnp.where(zl == q, row[:, q * width : (q + 1) * width], part)
    gradient[...] = part
    for o in range(1, n_z):
        column_copy(o).wait_send()


def to_tiles(array):
    *lead, ny, nz = array.shape
    split = array.reshape(*lead, ny // SUBLANES, SUBLANES, nz // LANES, LANES)
    return jnp.swapaxes(split, -2, -3).reshape(*lead[:-1], -1, LANES)


def from_tiles(array, shape):
    *lead, ny, nz = shape
    split = array.reshape(*lead, ny // SUBLANES, nz // LANES, SUBLANES, LANES)
    return jnp.swapaxes(split, -2, -3).reshape(shape)


def local(
    dims,
    adjoint,
    objective_gradient,
    diagonal,
    flux_blocks,
    flux_sensitivity,
    surface_mask,
    patch_band_slot,
    design_basis,
    condition_weights,
):
    _, nvar, nx, ny, nz = adjoint.shape
    rows = nx * ny
    n_cond, n_y, n_core, n_x, n_zl = dims
    n_plane, n_z = n_y * n_core * n_x, n_cond * n_zl
    f32 = jnp.float32
    flat = nx * ny * nz // LANES
    field, cell = (nvar, flat, LANES), (flat, LANES)
    anywhere = pl.BlockSpec(memory_space=pl.ANY)
    scalars = pl.BlockSpec(memory_space=pltpu.SMEM)
    vmem = pl.BlockSpec(memory_space=pltpu.VMEM)
    dma = pltpu.SemaphoreType.DMA
    smoothed, residual, gradient = pl.pallas_call(
        functools.partial(kernel, dims),
        out_shape=(
            jax.ShapeDtypeStruct(field, f32),
            jax.ShapeDtypeStruct(field, f32),
            jax.ShapeDtypeStruct((1, LANES // n_zl), f32),
        ),
        in_specs=[anywhere] * 6 + [scalars] * 2 + [vmem],
        out_specs=(vmem, vmem, vmem),
        scratch_shapes=[
            pltpu.VMEM(field, f32),
            pltpu.VMEM(field, f32),
            pltpu.VMEM(field, f32),
            pltpu.VMEM(cell, f32),
            pltpu.VMEM(cell, f32),
            pltpu.VMEM((nvar, rows, nz), jnp.bfloat16),
            pltpu.VMEM(cell, jnp.int32),
            pltpu.VMEM(design_basis.shape, f32),
            pltpu.VMEM((rows, nz), f32),
            pltpu.VMEM((3 * NDES // LANES, rows), f32),
            pltpu.VMEM((3, 2, nvar, ny * nz // LANES, LANES), f32),
            pltpu.VMEM((3, 2, nvar, nx * nz // LANES, LANES), f32),
            pltpu.VMEM((3, 2, nvar, nx * nz // LANES, LANES), f32),
            pltpu.VMEM((NDES // LANES, 1, LANES), f32),
            pltpu.VMEM((n_plane, 1, LANES), f32),
            pltpu.VMEM((1, 1, LANES), f32),
            pltpu.VMEM((n_z, 1, LANES), f32),
            dma((6,)),
            dma((3, 4)),
            dma((3, 4)),
            dma,
            dma,
            dma((n_z - 1,)),
            dma,
        ],
        compiler_params=pltpu.CompilerParams(
            collective_id=0, has_side_effects=True, vmem_limit_bytes=40 * 1024 * 1024
        ),
        name="adjoint_step",
    )(
        to_tiles(adjoint[0]),
        to_tiles(objective_gradient[0]),
        to_tiles(diagonal),
        flux_sensitivity.reshape(nvar, rows, nz),
        to_tiles(surface_mask),
        design_basis,
        flux_blocks,
        condition_weights,
        patch_band_slot,
    )
    whole = (1, nvar, nx, ny, nz)
    return from_tiles(smoothed, whole), from_tiles(residual, whole), gradient.reshape(-1)


def solution(mesh):
    dims = (mesh.shape["cond"], 4, 2, 4, 4)
    torus = Mesh(mesh.devices.reshape(dims), AXES)
    in_specs = (
        P("cond", None, GX, YZ, None),
        P("cond", None, GX, YZ, None),
        P(GX, YZ, None),
        P("cond", None, None, None),
        P("cond", None, GX, YZ, None),
        P(GX, YZ, None),
        P(GX, YZ),
        P(),
        P(),
    )
    out_specs = (P("cond", None, GX, YZ, None), P("cond", None, GX, YZ, None), P(GX_YZ))
    return jax.shard_map(
        functools.partial(local, dims), mesh=torus, in_specs=in_specs, out_specs=out_specs, check_vma=False
    )
```

time: 147 us -> 42 us (0.29)
  the two profiles are of different devices: /device:TPU:0 before, /device:TPU:1 now
where the time goes in v1:
time: 42 us; the launch traced here: 41.7 us
  Pallas kernels  32.1 us (76%)
  local copies, waits for them, and re-layouts  8.9 us (21%)
  between operations  0.67 us (2%)
    pallas_call x1, Pallas kernels, local(): pl.pallas_call(functools.partial(kernel, dims), out_shape=(jax.ShapeDtype...  32.1 us
    unnamed x20, local copies, waits for them, and re-layouts  8.9 us

profile of v1, /device:TPU:1, one launch (start us, length us, event | category | flops | bytes accessed | tf_op | source)
XLA Modules:
  0.0 41.7 jit_solution(14891098673516964352)
XLA Ops:
  0.6 0.0 copy-start.6
  0.6 0.0 copy-start.7
  0.7 0.8 %copy.12.blocks = f32[1,6,5,5]{3,2,1,0:T(8,128)S(1)} copy(f32[1,6,5,5]{1,0,3,2:T(1,128)} %param.12) | data formatting | bytes 1200 | tf_op args[3]
  1.5 0.0 copy-done.6
  1.5 0.0 copy-done.7
  1.5 0.0 copy-start
  1.5 1.1 %copy-done = f32[1,5,8,16,256]{4,3,2,1,0:T(8,128)S(1)} copy-done((f32[1,5,8,16,256]{4,3,2,1,0:T(8,128)S(1)}, f32[1,5,8,16,256]{4,3,2,1,0:T(8,128)}, u32[]{:S(2)}) %copy-start) | copy-done | bytes 655384
  2.6 0.0 copy-start.1
  2.6 1.1 %copy-done.1 = f32[1,5,8,16,256]{4,3,2,1,0:T(8,128)S(1)} copy-done((f32[1,5,8,16,256]{4,3,2,1,0:T(8,128)S(1)}, f32[1,5,8,16,256]{4,3,2,1,0:T(8,128)}, u32[]{:S(2)}) %copy-start.1) | copy-done | bytes 655384
  3.7 0.0 copy-start.2
  3.7 1.0 %copy-done.2 = bf16[1,5,8,16,256]{4,3,2,1,0:T(8,128)(2,1)S(1)} copy-done((bf16[1,5,8,16,256]{4,3,2,1,0:T(8,128)(2,1)S(1)}, bf16[1,5,8,16,256]{4,3,2,1,0:T(8,128)(2,1)}, u32[]{:S(2)}) %copy-start.2) | copy-done | bytes 327704
  4.7 0.0 copy-start.3
  4.7 0.9 %copy-done.3 = f32[8,16,256]{2,1,0:T(8,128)S(1)} copy-done((f32[8,16,256]{2,1,0:T(8,128)S(1)}, f32[8,16,256]{2,1,0:T(8,128)}, u32[]{:S(2)}) %copy-start.3) | copy-done | bytes 131096
  5.6 0.0 copy-start.4
  5.6 0.9 %copy-done.4 = s32[8,16,256]{2,1,0:T(8,128)S(1)} copy-done((s32[8,16,256]{2,1,0:T(8,128)S(1)}, s32[8,16,256]{2,1,0:T(8,128)}, u32[]{:S(2)}) %copy-start.4) | copy-done | bytes 131096
  6.5 0.0 copy-start.5
  6.5 0.9 %copy-done.5 = f32[256,128]{1,0:T(8,128)S(1)} copy-done((f32[256,128]{1,0:T(8,128)S(1)}, f32[256,128]{1,0:T(8,128)}, u32[]{:S(2)}) %copy-start.5) | copy-done | bytes 131096
  7.4 32.1 %adjoint_step.1 = (f32[5,256,128]{2,1,0:T(8,128)S(1)}, f32[5,256,128]{2,1,0:T(8,128)S(1)}, f32[1,32]{1,0:T(1,128)S(1)}) custom-call(f32[5,256,128]{2,1,0:T(8,128)S(1)} %bitcast.32, f32[5,256,128]{2,1,0:T(8,128)S(1)} %bitcast.33, f32[256,128]{1,0:T(8,128)S(1)} %bitcast.37, bf16[5,128,256]{2,1,0:T(8,128)(2,1)S(1)} %bitcast.36, s32[256,128]{1,0:T(8,128)S(1)} %bitcast.38, ...), custom_call_target="tpu_custom_call" | custom-call | tf_op jit(solution)/shard_map/adjoint_step/pallas_call | solution.py:456
  39.5 0.8 %copy.16 = f32[1,5,8,16,256]{4,3,2,1,0:T(8,128)} copy(f32[1,5,8,16,256]{4,3,2,1,0:T(8,128)S(1)} %bitcast.35) | data formatting | bytes 1310720
  40.3 0.8 %copy.17 = f32[1,5,8,16,256]{4,3,2,1,0:T(8,128)} copy(f32[1,5,8,16,256]{4,3,2,1,0:T(8,128)S(1)} %bitcast.34) | data formatting | bytes 1310720
  41.2 0.5 %copy.18 = f32[32]{0:T(128)} copy(f32[32]{0:T(128)S(1)} %bitcast.39) | data formatting | bytes 256
Async XLA Ops:
  0.6 0.9 %copy-start.6 = (s32[8,16]{1,0:T(8,128)S(1)}, s32[8,16]{1,0:T(8,128)}, u32[]{:S(2)}) copy-start(s32[8,16]{1,0:T(8,128)} %slots.1) | copy-start | bytes 1540
  0.6 0.9 %copy-start.7 = (s32[2]{0:T(128)S(1)}, s32[2]{0:T(128)}, u32[]{:S(2)}) copy-start(s32[2]{0:T(128)} %weights.1) | copy-start | bytes 28
  1.5 1.1 %copy-start = (f32[1,5,8,16,256]{4,3,2,1,0:T(8,128)S(1)}, f32[1,5,8,16,256]{4,3,2,1,0:T(8,128)}, u32[]{:S(2)}) copy-start(f32[1,5,8,16,256]{4,3,2,1,0:T(8,128)} %param.9) | copy-start | bytes 1966084
  2.6 1.1 %copy-start.1 = (f32[1,5,8,16,256]{4,3,2,1,0:T(8,128)S(1)}, f32[1,5,8,16,256]{4,3,2,1,0:T(8,128)}, u32[]{:S(2)}) copy-start(f32[1,5,8,16,256]{4,3,2,1,0:T(8,128)} %param.10) | copy-start | bytes 1966084
  3.7 1.0 %copy-start.2 = (bf16[1,5,8,16,256]{4,3,2,1,0:T(8,128)(2,1)S(1)}, bf16[1,5,8,16,256]{4,3,2,1,0:T(8,128)(2,1)}, u32[]{:S(2)}) copy-start(bf16[1,5,8,16,256]{4,3,2,1,0:T(8,128)(2,1)} %param.13) | copy-start | bytes 983044
  4.7 0.9 %copy-start.3 = (f32[8,16,256]{2,1,0:T(8,128)S(1)}, f32[8,16,256]{2,1,0:T(8,128)}, u32[]{:S(2)}) copy-start(f32[8,16,256]{2,1,0:T(8,128)} %param.11) | copy-start | bytes 393220
  5.6 0.9 %copy-start.4 = (s32[8,16,256]{2,1,0:T(8,128)S(1)}, s32[8,16,256]{2,1,0:T(8,128)}, u32[]{:S(2)}) copy-start(s32[8,16,256]{2,1,0:T(8,128)} %param.14) | copy-start | bytes 393220
  6.5 0.9 %copy-start.5 = (f32[256,128]{1,0:T(8,128)S(1)}, f32[256,128]{1,0:T(8,128)}, u32[]{:S(2)}) copy-start(f32[256,128]{1,0:T(8,128)} %basis.1) | copy-start | bytes 393220

commit v2 on v1

--- a/solution.py
+++ b/solution.py
@@ -18,6 +18,7 @@
 GX_YZ = GX + YZ
 MESH = pl.DeviceIdType.MESH
 RELAX = 0.8
+KERNEL_VMEM = 40 * 1024 * 1024
 X_HI, X_LO, Y_HI, Y_LO, Z_HI, Z_LO = range(6)
 
 
@@ -29,12 +30,15 @@
     sensitivity,
     mask,
     basis,
+    blocks_in,
+    weights_in,
+    slots_in,
+    smoothed,
+    residual,
+    gradient,
     blocks,
     weights,
     slots,
-    smoothed,
-    residual,
-    gradient,
     start,
     relaxed,
     source,
@@ -45,9 +49,12 @@
     base,
     surface,
     onehot,
+    mass,
     halo_x,
     halo_y,
+    face_x,
     face_y,
+    slots_beside,
     outgoing,
     plane_in,
     row_out,
@@ -55,6 +62,9 @@
     local_sem,
     halo_send,
     halo_recv,
+    slots_send,
+    slots_recv,
+    gate,
     plane_send,
     plane_recv,
     column_send,
@@ -72,17 +82,23 @@
     plane, z = gx * n_x + x, cond * n_zl + zl
 
     def at_gx(g):
-        return (cond, g // n_core, g % n_core, x, zl)
+        return (cond, lax.div(g, n_core), lax.rem(g, n_core), x, zl)
 
     def at_yz(q):
-        return (cond, y, core, q // n_zl, q % n_zl)
-
-    def at_plane(p):
-        g = p // n_x
-        return (cond, g // n_core, g % n_core, p % n_x, zl)
-
-    def at_z(q):
-        return (q // n_zl, y, core, x, q % n_zl)
+        return (cond, y, core, lax.div(q, n_zl), lax.rem(q, n_zl))
+
+    def around(index, size):
+        return [index] + [lax.rem(index + o, size) for o in range(1, size)]
+
+    conds, ys, cores, xs, zls = (around(i, n) for i, n in zip((cond, y, core, x, zl), dims))
+    plane_targets = [
+        ((cond, b, c, d, zl), (b * n_core + c) * n_x + d)
+        for i, b in enumerate(ys)
+        for j, c in enumerate(cores)
+        for k, d in enumerate(xs)
+        if i or j or k
+    ]
+    z_targets = [(a, y, core, x, e) for i, a in enumerate(conds) for j, e in enumerate(zls) if i or j]
 
     pairs = (
         (adjoint, start),
@@ -91,9 +107,12 @@
         (mask, surface_mask),
         (sensitivity, sens),
         (basis, base),
+        (blocks_in, blocks),
+        (weights_in, weights),
+        (slots_in, slots),
     )
     loads = [pltpu.make_async_copy(a, b, local_sem.at[i]) for i, (a, b) in enumerate(pairs)]
-    load_start, load_diag, load_source, load_mask, load_sens, load_base = loads
+    load_start, load_diag, load_source, load_mask, load_sens, load_base = loads[:6]
     for load in loads:
         load.start()
 
@@ -113,10 +132,13 @@
     def _():
         greet(at_yz(yz - 1))
 
-    for o in range(1, n_z):
-        greet(at_z((z + o) % n_z))
-    for o in range(1, n_plane):
-        greet(at_plane((plane + o) % n_plane))
+    line_gx = [(cond, b, c, x, zl) for i, b in enumerate(ys) for j, c in enumerate(cores) if i or j]
+    mirror = (n_cond - 1 - cond, y, core, x, n_zl - 1 - zl)
+    greeted = (
+        line_gx + [(cond, y, core, d, zl) for d in xs[1:]] + [(cond, y, core, x, e) for e in zls[1:]] + [mirror]
+    )
+    for target in greeted:
+        greet(target)
 
     sides = (
         (gx > 0, gx < n_gx - 1),
@@ -127,13 +149,17 @@
         for side in range(2):
 
             @pl.when(jnp.logical_not(sides[axis][side]))
-            def _(buffer=buffer, side=side):
+            def _(buffer=buffer, side=side, index=2 * axis + side):
                 buffer[:, side] = jnp.zeros_like(buffer[:, side])
+                slots_beside[index] = jnp.zeros_like(slots_beside[index])
 
     def halo_copy(field, turn, axis, side):
         index = 2 * axis + side
         if axis == 0:
-            src = field.at[:, pl.ds((nx - 1) * span if side else 0, span)]
+            if field is None:
+                src = face_x.at[side]
+            else:
+                src = field.at[:, pl.ds((nx - 1) * span if side else 0, span)]
             dst = halo_x.at[turn, 1 - side]
             target = at_gx(gx + 1 if side else gx - 1)
         else:
@@ -167,8 +193,52 @@
                 for c in range(n_col):
                     face_y[turn, side, e, pl.ds(c * nx, nx), :] = field[e, line(side, c), :]
 
+    far = (zl == 0, zl == n_zl - 1)
+
     def send_faces(field, turn):
-        each_side(lambda axis, side: halo_copy(field, turn, axis, side).start())
+        for side in range(2):
+
+            @pl.when(jnp.logical_and(sides[1][side], far[side]))
+            def _(side=side):
+                halo_copy(field, turn, 1, side).start()
+
+        for side in range(2):
+
+            @pl.when(jnp.logical_not(far[side]))
+            def _(side=side):
+                halo_copy(field, turn, 1, side).start()
+
+        for side in range(2):
+
+            @pl.when(sides[0][side])
+            def _(side=side):
+                halo_copy(field, turn, 0, side).start()
+
+    def slots_copy(axis, side):
+        index = 2 * axis + side
+        if axis == 0:
+            target = at_gx(gx + 1 if side else gx - 1)
+        else:
+            target = at_yz(yz + 1 if side else yz - 1)
+        return pltpu.make_async_remote_copy(
+            src_ref=slots,
+            dst_ref=slots_beside.at[2 * axis + 1 - side],
+            send_sem=slots_send.at[index],
+            recv_sem=slots_recv.at[2 * axis + 1 - side],
+            device_id=target,
+            device_id_type=MESH,
+        )
+
+    def wait_slots(axis, side):
+        index = 2 * axis + side
+        pltpu.make_async_remote_copy(
+            src_ref=slots,
+            dst_ref=slots_beside.at[index],
+            send_sem=slots_send.at[index],
+            recv_sem=slots_recv.at[index],
+            device_id=(cond, y, core, x, zl),
+            device_id_type=MESH,
+        ).wait_recv()
 
     def wait_faces(turn):
         def body(axis, side):
@@ -177,7 +247,7 @@
                 dst_ref=(halo_x if axis == 0 else halo_y).at[turn, side],
                 send_sem=halo_send.at[turn, 2 * axis + side],
                 recv_sem=halo_recv.at[turn, 2 * axis + side],
-                device_id=at_gx(gx) if axis == 0 else at_yz(yz),
+                device_id=(cond, y, core, x, zl),
                 device_id_type=MESH,
             ).wait_recv()
 
@@ -223,7 +293,7 @@
                 terms[d] = moved
             for d, values in terms.items():
                 for k in range(NVAR):
-                    coef = blocks[0, d, e, k]
+                    coef = blocks[e, k, 0, d]
                     for i, rc in enumerate(tiles):
                         part = coef * values[rc]
                         total[k][i] = part if total[k][i] is None else total[k][i] + part
@@ -263,76 +333,129 @@
 
         over_blocks(body)
 
+    def face_parts(axis, side):
+        if axis == 0:
+            first = (nx - 1) * span if side else 0
+            return [(pl.ds(first + i, SUBLANES), pl.ds(i, SUBLANES)) for i in range(0, span, SUBLANES)]
+        return [(line(side, c), pl.ds(c * nx, nx)) for c in range(n_col)]
+
     def add_halos(turn, result, scale):
         for axis, buffer in ((0, halo_x), (1, halo_y)):
             for side in range(2):
                 d = (X_LO, X_HI, Y_LO, Y_HI)[2 * axis + side]
-                if axis == 0:
-                    first = (nx - 1) * span if side else 0
-                    parts = [(pl.ds(first + i, SUBLANES), pl.ds(i, SUBLANES)) for i in range(0, span, SUBLANES)]
-                else:
-                    parts = [(line(side, c), pl.ds(c * nx, nx)) for c in range(n_col)]
-                for at, place in parts:
+                for at, place in face_parts(axis, side):
                     factor = None if scale is None else scale[at, :]
                     outside = [buffer[turn, side, e, place, :] for e in range(NVAR)]
                     for k in range(NVAR):
-                        part = blocks[0, d, 0, k] * outside[0]
+                        part = blocks[0, k, 0, d] * outside[0]
                         for e in range(1, NVAR):
-                            part = part + blocks[0, d, e, k] * outside[e]
+                            part = part + blocks[e, k, 0, d] * outside[e]
                         part = part if factor is None else factor * part
                         result[k, at, :] = result[k, at, :] + part
 
     load_start.wait()
     pack_faces(start, 0)
     pl.semaphore_wait(
-        barrier, n_z + n_plane - 2 + step_up.astype(jnp.int32) + step_down.astype(jnp.int32)
+        barrier, len(greeted) + step_up.astype(jnp.int32) + step_down.astype(jnp.int32)
     )
     send_faces(start, 0)
+
+    for load in loads[6:]:
+        load.wait()
+    each_side(lambda axis, side: slots_copy(axis, side).start())
+    for target in line_gx + [mirror]:
+        pl.semaphore_signal(gate, inc=1, device_id=target, device_id_type=MESH)
 
     load_diag.wait()
     ratio[...] = RELAX / diag[...]
+    load_mask.wait()
+    load_sens.wait()
+    for block in range(nx):
+        for c in range(n_col):
+            cols = pl.ds(c * LANES, LANES)
+            for k in range(NVAR):
+                weight = sens[k, pl.ds(block * ny, ny), cols].astype(jnp.float32)
+                for r in range(n_row):
+                    at = window(block, r, c)
+                    mass[k, at, :] = (
+                        surface_mask[at, :].astype(jnp.float32) * weight[r * SUBLANES : (r + 1) * SUBLANES]
+                    )
+    for axis, faces in ((1, face_y.at[3]), (0, face_x)):
+        for side in range(2):
+            d = (X_LO, X_HI, Y_LO, Y_HI)[2 * axis + side]
+            for at, place in face_parts(axis, side):
+                pull = [ratio[at, :] * mass[k, at, :] for k in range(NVAR)]
+                for e in range(NVAR):
+                    part = blocks[e, 0, 0, d] * pull[0]
+                    for k in range(1, NVAR):
+                        part = part + blocks[e, k, 0, d] * pull[k]
+                    faces[side, e, place, :] = part
+    send_faces(None, 3)
+
     load_source.wait()
     sweep(start, relaxed)
 
-    pick = lax.broadcasted_iota(jnp.int32, (ny, rows), 1) % ny == lax.broadcasted_iota(jnp.int32, (ny, rows), 0)
-    spread = jnp.dot(
-        slots[...].astype(jnp.float32), pick.astype(jnp.float32), preferred_element_type=jnp.float32
-    )
-    own = lax.broadcasted_iota(jnp.int32, (nx, rows), 1) // ny == lax.broadcasted_iota(jnp.int32, (nx, rows), 0)
-    slot_row = jnp.sum(jnp.where(own, spread, 0.0), axis=0, keepdims=True)
+    def number_of(shape, dim):
+        return lax.broadcasted_iota(jnp.int32, shape, dim)
+
+    def lookup(table, pick, keep):
+        spread = jnp.dot(
+            table.astype(jnp.float32), pick.astype(jnp.float32), preferred_element_type=jnp.float32
+        )
+        return jnp.sum(jnp.where(keep, spread, 0.0), axis=0, keepdims=True)
+
+    across, down = number_of((ny, rows), 1), number_of((ny, rows), 0)
+    lane, first = number_of((nx, rows), 1), number_of((nx, rows), 0)
+    slot_row = lookup(slots[...], lax.rem(across, ny) == down, lax.div(lane, ny) == first)
+    each_side(wait_slots)
+    beside_row = jnp.where(number_of((1, rows), 1) < 2 * (nx + ny), 0.0, -8.0)
+    for side in range(2):
+        base_lane = side * ny
+        beside_row = beside_row + lookup(
+            slots_beside[side],
+            across - base_lane == down,
+            first == (0 if side else nx - 1),
+        )
+        base_lane = 2 * ny + side * nx
+        beside_row = beside_row + lookup(
+            slots_beside[2 + side],
+            down == (0 if side else ny - 1),
+            lane - base_lane == first,
+        )
     n_out = NDES // LANES
-    number = lax.broadcasted_iota(jnp.int32, (3 * n_out, rows), 0)
-    third = number // n_out
-    wanted = 2 * (number % n_out) + jnp.where(third == 0, 0, jnp.where(third == 1, -1, 1))
-    onehot[...] = jnp.where(slot_row == wanted.astype(jnp.float32), 1.0, 0.0)
+    number = number_of((3 * n_out, rows), 0)
+    third = lax.div(number, n_out)
+    wanted = 2 * lax.rem(number, n_out) + jnp.where(third == 0, 0, jnp.where(third == 1, -1, 1))
+    onehot[:, :rows] = jnp.where(slot_row == wanted.astype(jnp.float32), 1.0, 0.0)
+    onehot[:, rows:] = jnp.where(beside_row == wanted.astype(jnp.float32), 1.0, 0.0)
+    surface[rows:, :] = jnp.zeros_like(surface[rows:, :])
+    load_base.wait()
 
     wait_faces(0)
     add_halos(0, relaxed, ratio)
     pack_faces(relaxed, 1)
     send_faces(relaxed, 1)
     sweep(relaxed, smoothed)
-    load_mask.wait()
-    load_sens.wait()
-    load_base.wait()
-    drain_faces(start, 0)
-
-    wait_faces(1)
-    add_halos(1, smoothed, ratio)
-    pack_faces(smoothed, 2)
-    send_faces(smoothed, 2)
 
     for block in range(nx):
-        for c in range(n_col):
-            cols = pl.ds(c * LANES, LANES)
-            weight = [sens[k, pl.ds(block * ny, ny), cols].astype(jnp.float32) for k in range(NVAR)]
-            for r in range(n_row):
-                at = window(block, r, c)
-                part = [
-                    smoothed[k, at, :] * weight[k][r * SUBLANES : (r + 1) * SUBLANES] for k in range(NVAR)
-                ]
-                surface[pl.ds(block * ny + r * SUBLANES, SUBLANES), cols] = surface_mask[at, :].astype(
-                    jnp.float32
-                ) * functools.reduce(jnp.add, part)
+        for r, c in tiles:
+            at = window(block, r, c)
+            part = [smoothed[k, at, :] * mass[k, at, :] for k in range(NVAR)]
+            surface[pl.ds(block * ny + r * SUBLANES, SUBLANES), pl.ds(c * LANES, LANES)] = functools.reduce(
+                jnp.add, part
+            )
+    wait_faces(3)
+    for axis, buffer in ((0, halo_x), (1, halo_y)):
+        for side in range(2):
+            for i, (at, place) in enumerate(face_parts(axis, side)):
+                part = [relaxed[e, at, :] * buffer[3, side, e, place, :] for e in range(NVAR)]
+                if axis == 0:
+                    to = rows + side * ny + (i // n_col) * SUBLANES
+                    c = i % n_col
+                else:
+                    to = rows + 2 * ny + side * nx
+                    c = i
+                surface[pl.ds(to, SUBLANES), pl.ds(c * LANES, LANES)] = functools.reduce(jnp.add, part)
     projected = jnp.dot(
         surface[...], base[...], precision=lax.Precision.HIGHEST, preferred_element_type=jnp.float32
     )
@@ -347,21 +470,29 @@
     scaled = (even + swapped) * (jnp.full((n_out, LANES), mine) / whole)
     outgoing[...] = scaled.reshape(n_out, 1, LANES)
 
-    def plane_copy(o):
-        target = (plane + o) % n_plane
+    def plane_copy(target, number):
         return pltpu.make_async_remote_copy(
-            src_ref=outgoing.at[target],
+            src_ref=outgoing.at[number],
             dst_ref=plane_in.at[plane],
             send_sem=plane_send,
             recv_sem=plane_recv,
-            device_id=at_plane(target),
+            device_id=target,
             device_id_type=MESH,
         )
 
-    for o in range(1, n_plane):
-        plane_copy(o).start()
+    pl.semaphore_wait(gate, len(line_gx) + 1)
+    for target, number in plane_targets:
+        plane_copy(target, number).start()
     plane_in[plane] = outgoing[plane]
 
+
+    wait_faces(1)
+    add_halos(1, smoothed, ratio)
+    pack_faces(smoothed, 2)
+    send_faces(smoothed, 2)
+    drain_faces(start, 0)
+    drain_faces(None, 3)
+    each_side(lambda axis, side: slots_copy(axis, side).wait_send())
     operate(smoothed, residual)
     drain_faces(relaxed, 1)
 
@@ -370,7 +501,7 @@
         dst_ref=plane_in.at[pl.ds(0, n_plane - 1)],
         send_sem=plane_send,
         recv_sem=plane_recv,
-        device_id=at_plane(plane),
+        device_id=(cond, y, core, x, zl),
         device_id_type=MESH,
     )
     everyone.wait_recv()
@@ -380,18 +511,18 @@
     row_out[0] = row
     column_in[z] = row
 
-    def column_copy(o):
+    def column_copy(i, target):
         return pltpu.make_async_remote_copy(
             src_ref=row_out.at[0],
             dst_ref=column_in.at[z],
-            send_sem=column_send.at[o - 1],
+            send_sem=column_send.at[i],
             recv_sem=column_recv,
-            device_id=at_z((z + o) % n_z),
+            device_id=target,
             device_id_type=MESH,
         )
 
-    for o in range(1, n_z):
-        column_copy(o).start()
+    for i, target in enumerate(z_targets):
+        column_copy(i, target).start()
 
     wait_faces(2)
     add_halos(2, residual, None)
@@ -403,7 +534,7 @@
         dst_ref=column_in.at[pl.ds(0, n_z - 1)],
         send_sem=column_send.at[0],
         recv_sem=column_recv,
-        device_id=at_z(z),
+        device_id=(cond, y, core, x, zl),
         device_id_type=MESH,
     ).wait_recv()
     row = column_in[0]
@@ -414,8 +545,17 @@
     for q in range(1, n_zl):
         part = jnp.where(zl == q, row[:, q * width : (q + 1) * width], part)
     gradient[...] = part
-    for o in range(1, n_z):
-        column_copy(o).wait_send()
+    for i, target in enumerate(z_targets):
+        column_copy(i, target).wait_send()
+
+
+def put_out(*refs):
+    count = (len(refs) - 1) // 2
+    copies = [pltpu.make_async_copy(refs[i], refs[count + i], refs[-1].at[i]) for i in range(count)]
+    for copy in copies:
+        copy.start()
+    for copy in copies:
+        copy.wait()
 
 
 def to_tiles(array):
@@ -449,8 +589,7 @@
     f32 = jnp.float32
     flat = nx * ny * nz // LANES
     field, cell = (nvar, flat, LANES), (flat, LANES)
-    anywhere = pl.BlockSpec(memory_space=pl.ANY)
-    scalars = pl.BlockSpec(memory_space=pltpu.SMEM)
+    hbm = pl.BlockSpec(memory_space=pltpu.HBM)
     vmem = pl.BlockSpec(memory_space=pltpu.VMEM)
     dma = pltpu.SemaphoreType.DMA
     smoothed, residual, gradient = pl.pallas_call(
@@ -460,9 +599,12 @@
             jax.ShapeDtypeStruct(field, f32),
             jax.ShapeDtypeStruct((1, LANES // n_zl), f32),
         ),
-        in_specs=[anywhere] * 6 + [scalars] * 2 + [vmem],
+        in_specs=[hbm] * 9,
         out_specs=(vmem, vmem, vmem),
         scratch_shapes=[
+            pltpu.SMEM((nvar, nvar, 1, 6), f32),
+            pltpu.SMEM((n_cond,), jnp.int32),
+            pltpu.VMEM((nx, ny), jnp.int32),
             pltpu.VMEM(field, f32),
             pltpu.VMEM(field, f32),
             pltpu.VMEM(field, f32),
@@ -471,38 +613,59 @@
             pltpu.VMEM((nvar, rows, nz), jnp.bfloat16),
             pltpu.VMEM(cell, jnp.int32),
             pltpu.VMEM(design_basis.shape, f32),
-            pltpu.VMEM((rows, nz), f32),
-            pltpu.VMEM((3 * NDES // LANES, rows), f32),
-            pltpu.VMEM((3, 2, nvar, ny * nz // LANES, LANES), f32),
-            pltpu.VMEM((3, 2, nvar, nx * nz // LANES, LANES), f32),
-            pltpu.VMEM((3, 2, nvar, nx * nz // LANES, LANES), f32),
+            pltpu.VMEM((2 * rows, nz), f32),
+            pltpu.VMEM((3 * NDES // LANES, 2 * rows), f32),
+            pltpu.VMEM(field, f32),
+            pltpu.VMEM((4, 2, nvar, ny * nz // LANES, LANES), f32),
+            pltpu.VMEM((4, 2, nvar, nx * nz // LANES, LANES), f32),
+            pltpu.VMEM((2, nvar, ny * nz // LANES, LANES), f32),
+            pltpu.VMEM((4, 2, nvar, nx * nz // LANES, LANES), f32),
+            pltpu.VMEM((4, nx, ny), jnp.int32),
             pltpu.VMEM((NDES // LANES, 1, LANES), f32),
             pltpu.VMEM((n_plane, 1, LANES), f32),
             pltpu.VMEM((1, 1, LANES), f32),
             pltpu.VMEM((n_z, 1, LANES), f32),
-            dma((6,)),
-            dma((3, 4)),
-            dma((3, 4)),
+            dma((9,)),
+            dma((4, 4)),
+            dma((4, 4)),
+            dma((4,)),
+            dma((4,)),
+            pltpu.SemaphoreType.REGULAR,
             dma,
             dma,
             dma((n_z - 1,)),
             dma,
         ],
         compiler_params=pltpu.CompilerParams(
-            collective_id=0, has_side_effects=True, vmem_limit_bytes=40 * 1024 * 1024
+            collective_id=0, has_side_effects=True, vmem_limit_bytes=KERNEL_VMEM
         ),
         name="adjoint_step",
     )(
-        to_tiles(adjoint[0]),
-        to_tiles(objective_gradient[0]),
-        to_tiles(diagonal),
-        flux_sensitivity.reshape(nvar, rows, nz),
-        to_tiles(surface_mask),
-        design_basis,
-        flux_blocks,
-        condition_weights,
-        patch_band_slot,
-    )
+        *(
+            pltpu.with_memory_space_constraint(a, pltpu.HBM)
+            for a in (
+                to_tiles(adjoint[0]),
+                to_tiles(objective_gradient[0]),
+                to_tiles(diagonal),
+                flux_sensitivity.reshape(nvar, rows, nz),
+                to_tiles(surface_mask),
+                design_basis,
+                jnp.transpose(flux_blocks, (2, 3, 0, 1)),
+                condition_weights,
+                patch_band_slot,
+            )
+        )
+    )
+    results = (smoothed, residual, gradient)
+    smoothed, residual, gradient = pl.pallas_call(
+        put_out,
+        out_shape=tuple(jax.ShapeDtypeStruct(a.shape, a.dtype) for a in results),
+        in_specs=[vmem] * 3,
+        out_specs=(hbm,) * 3,
+        scratch_shapes=[dma((3,))],
+        compiler_params=pltpu.CompilerParams(vmem_limit_bytes=4 * 1024 * 1024),
+        name="put_out",
+    )(*results)
     whole = (1, nvar, nx, ny, nz)
     return from_tiles(smoothed, whole), from_tiles(residual, whole), gradient.reshape(-1)
 

time: 42 us -> 30 us (0.71)
  local copies, waits for them, and re-layouts: 8.9 us -> 0 us
  Pallas kernels: 32.1 us -> 29.3 us
    unnamed x20 -> x0, local copies, waits for them, and re-layouts: 8.9 us -> none
    pallas_call x1, Pallas kernels: 32.1 us -> 28.2 us  [local(): pl.pallas_call(functools.partial(kernel, dims), out_shape=(jax.ShapeDtype...]
    pallas_call x0 -> x1, Pallas kernels: none -> 1.08 us  [local(): pl.pallas_call(put_out, out_shape=tuple((jax.ShapeDtypeStruct(a.shape, a....]
where the time goes in v2:
time: 30 us; the launch traced here: 29.9 us
  Pallas kernels  29.3 us (98%)
  between operations  0.64 us (2%)
    pallas_call x1, Pallas kernels, local(): pl.pallas_call(functools.partial(kernel, dims), out_shape=(jax.ShapeDtype...  28.2 us
    pallas_call x1, Pallas kernels, local(): pl.pallas_call(put_out, out_shape=tuple((jax.ShapeDtypeStruct(a.shape, a....  1.08 us

profile of v2, /device:TPU:1, one launch (start us, length us, event | category | flops | bytes accessed | tf_op | source)
XLA Modules:
  0.0 29.9 jit_solution(17638286430262478685)
XLA Ops:
  0.6 28.2 %adjoint_step.1 = (f32[5,256,128]{2,1,0:T(8,128)S(1)}, f32[5,256,128]{2,1,0:T(8,128)S(1)}, f32[1,32]{1,0:T(1,128)S(1)}) custom-call(f32[5,256,128]{2,1,0:T(8,128)} %bitcast.33, f32[5,256,128]{2,1,0:T(8,128)} %bitcast.34, f32[256,128]{1,0:T(8,128)} %bitcast.36, bf16[5,128,256]{2,1,0:T(8,128)(2,1)} %bitcast.35, s32[256,128]{1,0:T(8,128)} %bitcast.37, ...), custom_call_target="tpu_custom_call" | custom-call | tf_op jit(solution)/shard_map/adjoint_step/pallas_call | solution.py:595
  28.8 1.1 %put_out.1 = (f32[5,256,128]{2,1,0:T(8,128)}, f32[5,256,128]{2,1,0:T(8,128)}, f32[1,32]{1,0:T(1,128)}) custom-call(f32[5,256,128]{2,1,0:T(8,128)S(1)} %get-tuple-element.9.refs_0_, f32[5,256,128]{2,1,0:T(8,128)S(1)} %get-tuple-element.10.refs_1_, f32[1,32]{1,0:T(1,128)S(1)} %get-tuple-element.11.refs_2_), custom_call_target="tpu_custom_call" | custom-call | tf_op jit(solution)/shard_map/put_out/pallas_call | solution.py:660

commit v3 on v2

--- a/solution.py
+++ b/solution.py
@@ -49,7 +49,10 @@
     base,
     surface,
     onehot,
+    base_parts,
     mass,
+    pulls,
+    fixed,
     halo_x,
     halo_y,
     face_x,
@@ -91,14 +94,45 @@
         return [index] + [lax.rem(index + o, size) for o in range(1, size)]
 
     conds, ys, cores, xs, zls = (around(i, n) for i, n in zip((cond, y, core, x, zl), dims))
-    plane_targets = [
-        ((cond, b, c, d, zl), (b * n_core + c) * n_x + d)
-        for i, b in enumerate(ys)
-        for j, c in enumerate(cores)
-        for k, d in enumerate(xs)
-        if i or j or k
+    steps = [
+        (i, j, k, l)
+        for i in range(n_cond)
+        for j in range(n_y)
+        for k in range(n_x)
+        for l in range(n_zl)
+        if i or j or k or l
     ]
-    z_targets = [(a, y, core, x, e) for i, a in enumerate(conds) for j, e in enumerate(zls) if i or j]
+    steps.sort(key=lambda s: -(min(s[1], n_y - s[1]) + min(s[2], n_x - s[2]) + (n_zl if s[0] else s[3])))
+    chip_targets = [
+        ((conds[i], ys[j], core, xs[k], zls[l]), zls[l] * n_y * n_x + ys[j] * n_x + xs[k])
+        for i, j, k, l in steps
+    ]
+    n_chips = len(steps) + 1
+    chip = (cond * n_zl + zl) * n_y * n_x + y * n_x + x
+
+    barrier = pltpu.get_barrier_semaphore()
+
+    def greet(target):
+        pl.semaphore_signal(barrier, inc=1, device_id=target, device_id_type=MESH)
+
+    step_up = jnp.logical_and(zl == n_zl - 1, x < n_x - 1)
+    step_down = jnp.logical_and(zl == 0, x > 0)
+
+    @pl.when(step_up)
+    def _():
+        greet(at_yz(yz + 1))
+
+    @pl.when(step_down)
+    def _():
+        greet(at_yz(yz - 1))
+
+    line_gx = [(cond, b, c, x, zl) for i, b in enumerate(ys) for j, c in enumerate(cores) if i or j]
+    mirror = (n_cond - 1 - cond, y, core, x, n_zl - 1 - zl)
+    greeted = (
+        line_gx + [(cond, y, core, d, zl) for d in xs[1:]] + [(cond, y, core, x, e) for e in zls[1:]] + [mirror]
+    )
+    for target in greeted:
+        greet(target)
 
     pairs = (
         (adjoint, start),
@@ -115,30 +149,6 @@
     load_start, load_diag, load_source, load_mask, load_sens, load_base = loads[:6]
     for load in loads:
         load.start()
-
-    barrier = pltpu.get_barrier_semaphore()
-
-    def greet(target):
-        pl.semaphore_signal(barrier, inc=1, device_id=target, device_id_type=MESH)
-
-    step_up = jnp.logical_and(zl == n_zl - 1, x < n_x - 1)
-    step_down = jnp.logical_and(zl == 0, x > 0)
-
-    @pl.when(step_up)
-    def _():
-        greet(at_yz(yz + 1))
-
-    @pl.when(step_down)
-    def _():
-        greet(at_yz(yz - 1))
-
-    line_gx = [(cond, b, c, x, zl) for i, b in enumerate(ys) for j, c in enumerate(cores) if i or j]
-    mirror = (n_cond - 1 - cond, y, core, x, n_zl - 1 - zl)
-    greeted = (
-        line_gx + [(cond, y, core, d, zl) for d in xs[1:]] + [(cond, y, core, x, e) for e in zls[1:]] + [mirror]
-    )
-    for target in greeted:
-        greet(target)
 
     sides = (
         (gx > 0, gx < n_gx - 1),
@@ -262,11 +272,20 @@
         at = block * span + (r * n_col + c) * SUBLANES
         return pl.ds(at if isinstance(at, int) else pl.multiple_of(at, SUBLANES), SUBLANES)
 
+    def moved(here, d):
+        axis, size, up = (0 if d in (Y_HI, Y_LO) else 1), (SUBLANES if d in (Y_HI, Y_LO) else LANES), d in (Y_HI, Z_HI)
+        index = lax.broadcasted_iota(jnp.int32, (SUBLANES, LANES), axis)
+        zero = jnp.zeros((SUBLANES, LANES), jnp.float32)
+        edge, shift, step = (size - 1, size - 1, 1) if up else (0, 1, -1)
+        turned = {rc: pltpu.roll(here[rc], shift, axis) for rc in tiles}
+        return {
+            (r, c): jnp.where(
+                index == edge, turned.get((r + step, c) if axis == 0 else (r, c + step), zero), turned[r, c]
+            )
+            for r, c in tiles
+        }
+
     def neighbours(field, block, lo, hi):
-        sub = lax.broadcasted_iota(jnp.int32, (SUBLANES, LANES), 0)
-        lane = lax.broadcasted_iota(jnp.int32, (SUBLANES, LANES), 1)
-        zero = jnp.zeros((SUBLANES, LANES), jnp.float32)
-
         def tile_of(e, b, r, c):
             return field[e, window(b, r, c), :]
 
@@ -278,19 +297,8 @@
                 terms[X_HI] = {rc: tile_of(e, block + 1, *rc) for rc in tiles}
             if lo:
                 terms[X_LO] = {rc: tile_of(e, block - 1, *rc) for rc in tiles}
-            for d, shift, axis, index, edge in (
-                (Y_HI, SUBLANES - 1, 0, sub, SUBLANES - 1),
-                (Y_LO, 1, 0, sub, 0),
-                (Z_HI, LANES - 1, 1, lane, LANES - 1),
-                (Z_LO, 1, 1, lane, 0),
-            ):
-                turned = {rc: pltpu.roll(here[rc], shift, axis) for rc in tiles}
-                step = 1 if edge else -1
-                moved = {}
-                for r, c in tiles:
-                    beside = (r + step, c) if axis == 0 else (r, c + step)
-                    moved[r, c] = jnp.where(index == edge, turned.get(beside, zero), turned[r, c])
-                terms[d] = moved
+            for d in (Y_HI, Y_LO, Z_HI, Z_LO):
+                terms[d] = moved(here, d)
             for d, values in terms.items():
                 for k in range(NVAR):
                     coef = blocks[e, k, 0, d]
@@ -299,17 +307,22 @@
                         total[k][i] = part if total[k][i] is None else total[k][i] + part
         return total
 
-    def over_blocks(body):
+    def over_blocks(body, between=None):
         body(0, False, True)
 
         def inner(b, carry):
             body(b, True, True)
             return carry
 
-        lax.fori_loop(1, nx - 1, inner, 0)
+        if between is None:
+            lax.fori_loop(1, nx - 1, inner, 0)
+        else:
+            lax.fori_loop(1, nx - 2, inner, 0)
+            between()
+            lax.fori_loop(nx - 2, nx - 1, inner, 0)
         body(nx - 1, True, False)
 
-    def sweep(field, result):
+    def sweep(field, result, between=None):
         def body(block, lo, hi):
             total = neighbours(field, block, lo, hi)
             for i, rc in enumerate(tiles):
@@ -320,7 +333,7 @@
                         source[k, at, :] + total[k][i]
                     )
 
-        over_blocks(body)
+        over_blocks(body, between)
 
     def operate(field, result):
         def body(block, lo, hi):
@@ -355,17 +368,8 @@
 
     load_start.wait()
     pack_faces(start, 0)
-    pl.semaphore_wait(
-        barrier, len(greeted) + step_up.astype(jnp.int32) + step_down.astype(jnp.int32)
-    )
-    send_faces(start, 0)
-
     for load in loads[6:]:
         load.wait()
-    each_side(lambda axis, side: slots_copy(axis, side).start())
-    for target in line_gx + [mirror]:
-        pl.semaphore_signal(gate, inc=1, device_id=target, device_id_type=MESH)
-
     load_diag.wait()
     ratio[...] = RELAX / diag[...]
     load_mask.wait()
@@ -390,10 +394,61 @@
                     for k in range(1, NVAR):
                         part = part + blocks[e, k, 0, d] * pull[k]
                     faces[side, e, place, :] = part
+    pl.semaphore_wait(
+        barrier, len(greeted) + step_up.astype(jnp.int32) + step_down.astype(jnp.int32)
+    )
+    send_faces(start, 0)
+    each_side(lambda axis, side: slots_copy(axis, side).start())
+    line_zl = [(cond, y, core, x, e) for e in zls[1:]]
+
+    def open_gate(i, targets):
+        for target in targets:
+            pl.semaphore_signal(gate.at[i], inc=1, device_id=target, device_id_type=MESH)
+
+    open_gate(0, line_gx)
+
     send_faces(None, 3)
 
     load_source.wait()
-    sweep(start, relaxed)
+
+    def second_gate():
+        pl.semaphore_wait(gate.at[0], len(line_gx))
+        open_gate(1, line_zl)
+
+    sweep(start, relaxed, second_gate)
+
+    def weigh(block, carry):
+        pull = []
+        for k in range(NVAR):
+            pull.append({rc: ratio[window(block, *rc), :] * mass[k, window(block, *rc), :] for rc in tiles})
+        for rc in tiles:
+            at = window(block, *rc)
+            part = [pull[k][rc] * source[k, at, :] for k in range(NVAR)]
+            fixed[at, :] = functools.reduce(jnp.add, part)
+        for d in range(6):
+            for e in range(NVAR):
+                line_of = {}
+                for rc in tiles:
+                    part = blocks[e, 0, 0, d] * pull[0][rc]
+                    for k in range(1, NVAR):
+                        part = part + blocks[e, k, 0, d] * pull[k][rc]
+                    line_of[rc] = part
+                if d in (Y_HI, Y_LO, Z_HI, Z_LO):
+                    line_of = moved(line_of, {Y_HI: Y_LO, Y_LO: Y_HI, Z_HI: Z_LO, Z_LO: Z_HI}[d])
+                for rc in tiles:
+                    pulls[d, e, window(block, *rc), :] = line_of[rc]
+        return carry
+
+    lax.fori_loop(0, nx, weigh, 0)
+    pl.semaphore_wait(gate.at[1], len(line_zl))
+    open_gate(2, [mirror])
+
+    def two_parts(value):
+        high = value.astype(jnp.bfloat16)
+        return high, (value - high.astype(jnp.float32)).astype(jnp.bfloat16)
+
+    def multiply(a, b):
+        return jnp.dot(a, b, preferred_element_type=jnp.float32)
 
     def number_of(shape, dim):
         return lax.broadcasted_iota(jnp.int32, shape, dim)
@@ -425,25 +480,44 @@
     n_out = NDES // LANES
     number = number_of((3 * n_out, rows), 0)
     third = lax.div(number, n_out)
-    wanted = 2 * lax.rem(number, n_out) + jnp.where(third == 0, 0, jnp.where(third == 1, -1, 1))
-    onehot[:, :rows] = jnp.where(slot_row == wanted.astype(jnp.float32), 1.0, 0.0)
-    onehot[:, rows:] = jnp.where(beside_row == wanted.astype(jnp.float32), 1.0, 0.0)
+    place = lax.rem(number, n_out)
+    half_out = n_out // n_core
+    row_of = (lax.div(lax.rem(place, half_out), n_x) * n_core + lax.div(place, half_out)) * n_x + lax.rem(place, n_x)
+    wanted = 2 * row_of + jnp.where(third == 0, 0, jnp.where(third == 1, -1, 1))
+    onehot[:, :rows] = jnp.where(slot_row == wanted.astype(jnp.float32), 1.0, 0.0).astype(jnp.bfloat16)
+    onehot[:, rows:] = jnp.where(beside_row == wanted.astype(jnp.float32), 1.0, 0.0).astype(jnp.bfloat16)
     surface[rows:, :] = jnp.zeros_like(surface[rows:, :])
     load_base.wait()
+    base_parts[0], base_parts[1] = two_parts(base[...])
 
     wait_faces(0)
     add_halos(0, relaxed, ratio)
     pack_faces(relaxed, 1)
     send_faces(relaxed, 1)
-    sweep(relaxed, smoothed)
-
-    for block in range(nx):
+    def add_surface(block, lo, hi):
+        total = {}
+        for rc in tiles:
+            at = window(block, *rc)
+            part = [fixed[at, :]]
+            part += [(1.0 - RELAX) * mass[e, at, :] * relaxed[e, at, :] for e in range(NVAR)]
+            for d, exists, step in ((X_HI, hi, 1), (X_LO, lo, -1)):
+                if exists:
+                    part += [pulls[d, e, at, :] * relaxed[e, window(block + step, *rc), :] for e in range(NVAR)]
+            total[rc] = functools.reduce(jnp.add, part)
+        for d in (Y_HI, Y_LO, Z_HI, Z_LO):
+            line_of = {}
+            for rc in tiles:
+                at = window(block, *rc)
+                part = [pulls[d, e, at, :] * relaxed[e, at, :] for e in range(NVAR)]
+                line_of[rc] = functools.reduce(jnp.add, part)
+            line_of = moved(line_of, d)
+            total = {rc: total[rc] + line_of[rc] for rc in tiles}
         for r, c in tiles:
-            at = window(block, r, c)
-            part = [smoothed[k, at, :] * mass[k, at, :] for k in range(NVAR)]
-            surface[pl.ds(block * ny + r * SUBLANES, SUBLANES), pl.ds(c * LANES, LANES)] = functools.reduce(
-                jnp.add, part
-            )
+            at = block * ny + r * SUBLANES
+            at = at if isinstance(at, int) else pl.multiple_of(at, SUBLANES)
+            surface[pl.ds(at, SUBLANES), pl.ds(c * LANES, LANES)] = total[r, c]
+
+    over_blocks(add_surface)
     wait_faces(3)
     for axis, buffer in ((0, halo_x), (1, halo_y)):
         for side in range(2):
@@ -456,12 +530,12 @@
                     to = rows + 2 * ny + side * nx
                     c = i
                 surface[pl.ds(to, SUBLANES), pl.ds(c * LANES, LANES)] = functools.reduce(jnp.add, part)
-    projected = jnp.dot(
-        surface[...], base[...], precision=lax.Precision.HIGHEST, preferred_element_type=jnp.float32
-    )
-    looked = jnp.dot(
-        onehot[...], projected, precision=lax.Precision.HIGHEST, preferred_element_type=jnp.float32
-    )
+    high, low = two_parts(surface[...])
+    projected = (
+        multiply(high, base_parts[1]) + multiply(low, base_parts[0])
+    ) + multiply(high, base_parts[0])
+    high, low = two_parts(projected)
+    looked = multiply(onehot[...], high) + multiply(onehot[...], low)
     even, before, after = (looked[i * n_out : (i + 1) * n_out] for i in range(3))
     half = lax.broadcasted_iota(jnp.int32, (n_out, LANES), 1) < LANES // 2
     swapped = pltpu.roll(jnp.where(half, after, before), LANES // 2, 1)
@@ -470,21 +544,39 @@
     scaled = (even + swapped) * (jnp.full((n_out, LANES), mine) / whole)
     outgoing[...] = scaled.reshape(n_out, 1, LANES)
 
-    def plane_copy(target, number):
+    half = pl.ds(core * half_out, half_out)
+    other = pl.ds((1 - core) * half_out, half_out)
+    pair = pltpu.make_async_remote_copy(
+        src_ref=outgoing.at[other],
+        dst_ref=plane_in,
+        send_sem=plane_send,
+        recv_sem=plane_recv,
+        device_id=(cond, y, 1 - core, x, zl),
+        device_id_type=MESH,
+    )
+    pair.start()
+    pl.semaphore_wait(gate.at[2], 1)
+    pair.wait()
+    width = LANES // n_zl
+    summed = (outgoing[half] + plane_in[...]).reshape(half_out, LANES)
+    for q in range(n_zl):
+        quarter = summed if q == 0 else pltpu.roll(summed, LANES - q * width, 1)
+        row_out[pl.ds(q * half_out, half_out)] = quarter[:, :width].reshape(half_out, 1, width)
+
+    def chip_copy(target, number):
         return pltpu.make_async_remote_copy(
-            src_ref=outgoing.at[number],
-            dst_ref=plane_in.at[plane],
-            send_sem=plane_send,
-            recv_sem=plane_recv,
+            src_ref=row_out.at[number],
+            dst_ref=column_in.at[chip],
+            send_sem=column_send,
+            recv_sem=column_recv,
             device_id=target,
             device_id_type=MESH,
         )
 
-    pl.semaphore_wait(gate, len(line_gx) + 1)
-    for target, number in plane_targets:
-        plane_copy(target, number).start()
-    plane_in[plane] = outgoing[plane]
-
+    for target, number in chip_targets:
+        chip_copy(target, number).start()
+    column_in[chip] = row_out[zl * n_y * n_x + y * n_x + x]
+    sweep(relaxed, smoothed)
 
     wait_faces(1)
     add_halos(1, smoothed, ratio)
@@ -496,57 +588,26 @@
     operate(smoothed, residual)
     drain_faces(relaxed, 1)
 
-    everyone = pltpu.make_async_remote_copy(
-        src_ref=outgoing.at[pl.ds(0, n_plane - 1)],
-        dst_ref=plane_in.at[pl.ds(0, n_plane - 1)],
-        send_sem=plane_send,
-        recv_sem=plane_recv,
-        device_id=(cond, y, core, x, zl),
-        device_id_type=MESH,
-    )
-    everyone.wait_recv()
-    row = plane_in[0]
-    for i in range(1, n_plane):
-        row = row + plane_in[i]
-    row_out[0] = row
-    column_in[z] = row
-
-    def column_copy(i, target):
-        return pltpu.make_async_remote_copy(
-            src_ref=row_out.at[0],
-            dst_ref=column_in.at[z],
-            send_sem=column_send.at[i],
-            recv_sem=column_recv,
-            device_id=target,
-            device_id_type=MESH,
-        )
-
-    for i, target in enumerate(z_targets):
-        column_copy(i, target).start()
-
     wait_faces(2)
     add_halos(2, residual, None)
-    everyone.wait_send()
     drain_faces(smoothed, 2)
 
-    pltpu.make_async_remote_copy(
-        src_ref=column_in.at[pl.ds(0, n_z - 1)],
-        dst_ref=column_in.at[pl.ds(0, n_z - 1)],
-        send_sem=column_send.at[0],
+    everyone = pltpu.make_async_remote_copy(
+        src_ref=column_in.at[pl.ds(0, n_chips - 1)],
+        dst_ref=column_in.at[pl.ds(0, n_chips - 1)],
+        send_sem=column_send,
         recv_sem=column_recv,
         device_id=(cond, y, core, x, zl),
         device_id_type=MESH,
-    ).wait_recv()
-    row = column_in[0]
-    for i in range(1, n_z):
-        row = row + column_in[i]
-    width = LANES // n_zl
-    part = row[:, :width]
-    for q in range(1, n_zl):
-        part = jnp.where(zl == q, row[:, q * width : (q + 1) * width], part)
-    gradient[...] = part
-    for i, target in enumerate(z_targets):
-        column_copy(i, target).wait_send()
+    )
+    everyone.wait_recv()
+    groups = 8
+    sums = [column_in[i] for i in range(groups)]
+    for i in range(groups, n_chips):
+        sums[i % groups] = sums[i % groups] + column_in[i]
+    row = functools.reduce(jnp.add, sums)
+    gradient[...] = row
+    everyone.wait_send()
 
 
 def put_out(*refs):
@@ -614,26 +675,29 @@
             pltpu.VMEM(cell, jnp.int32),
             pltpu.VMEM(design_basis.shape, f32),
             pltpu.VMEM((2 * rows, nz), f32),
-            pltpu.VMEM((3 * NDES // LANES, 2 * rows), f32),
+            pltpu.VMEM((3 * NDES // LANES, 2 * rows), jnp.bfloat16),
+            pltpu.VMEM((2, *design_basis.shape), jnp.bfloat16),
             pltpu.VMEM(field, f32),
+            pltpu.VMEM((6, *field), f32),
+            pltpu.VMEM(cell, f32),
             pltpu.VMEM((4, 2, nvar, ny * nz // LANES, LANES), f32),
             pltpu.VMEM((4, 2, nvar, nx * nz // LANES, LANES), f32),
             pltpu.VMEM((2, nvar, ny * nz // LANES, LANES), f32),
             pltpu.VMEM((4, 2, nvar, nx * nz // LANES, LANES), f32),
             pltpu.VMEM((4, nx, ny), jnp.int32),
             pltpu.VMEM((NDES // LANES, 1, LANES), f32),
-            pltpu.VMEM((n_plane, 1, LANES), f32),
-            pltpu.VMEM((1, 1, LANES), f32),
-            pltpu.VMEM((n_z, 1, LANES), f32),
+            pltpu.VMEM((n_y * n_x, 1, LANES), f32),
+            pltpu.VMEM((n_zl * n_y * n_x, 1, LANES // n_zl), f32),
+            pltpu.VMEM((n_cond * n_zl * n_y * n_x, 1, LANES // n_zl), f32),
             dma((9,)),
             dma((4, 4)),
             dma((4, 4)),
             dma((4,)),
             dma((4,)),
-            pltpu.SemaphoreType.REGULAR,
+            pltpu.SemaphoreType.REGULAR((3,)),
             dma,
             dma,
-            dma((n_z - 1,)),
+            dma,
             dma,
         ],
         compiler_params=pltpu.CompilerParams(

time: 30 us -> 27.5 us (0.917)
  Pallas kernels: 29.3 us -> 26.7 us
    pallas_call x1, Pallas kernels: 28.2 us -> 25.7 us  [local(): pl.pallas_call(functools.partial(kernel, dims), out_shape=(jax.ShapeDtype...]
where the time goes in v3:
time: 27.5 us; the launch traced here: 27.4 us
  Pallas kernels  26.7 us (97%)
  between operations  0.64 us (2%)
    pallas_call x1, Pallas kernels, local(): pl.pallas_call(functools.partial(kernel, dims), out_shape=(jax.ShapeDtype...  25.7 us
    pallas_call x1, Pallas kernels, local(): pl.pallas_call(put_out, out_shape=tuple((jax.ShapeDtypeStruct(a.shape, a....  1.08 us

profile of v3, /device:TPU:1, one launch (start us, length us, event | category | flops | bytes accessed | tf_op | source)
XLA Modules:
  0.0 27.4 jit_solution(3119799856520000685)
XLA Ops:
  0.6 25.7 %adjoint_step.1 = (f32[5,256,128]{2,1,0:T(8,128)S(1)}, f32[5,256,128]{2,1,0:T(8,128)S(1)}, f32[1,32]{1,0:T(1,128)S(1)}) custom-call(f32[5,256,128]{2,1,0:T(8,128)} %bitcast.33, f32[5,256,128]{2,1,0:T(8,128)} %bitcast.34, f32[256,128]{1,0:T(8,128)} %bitcast.36, bf16[5,128,256]{2,1,0:T(8,128)(2,1)} %bitcast.35, s32[256,128]{1,0:T(8,128)} %bitcast.37, ...), custom_call_target="tpu_custom_call" | custom-call | tf_op jit(solution)/shard_map/adjoint_step/pallas_call | solution.py:656
  26.3 1.1 %put_out.1 = (f32[5,256,128]{2,1,0:T(8,128)}, f32[5,256,128]{2,1,0:T(8,128)}, f32[1,32]{1,0:T(1,128)}) custom-call(f32[5,256,128]{2,1,0:T(8,128)S(1)} %get-tuple-element.9.refs_0_, f32[5,256,128]{2,1,0:T(8,128)S(1)} %get-tuple-element.10.refs_1_, f32[1,32]{1,0:T(1,128)S(1)} %get-tuple-element.11.refs_2_), custom_call_target="tpu_custom_call" | custom-call | tf_op jit(solution)/shard_map/put_out/pallas_call | solution.py:724

commit v4 on v3

--- a/solution.py
+++ b/solution.py
@@ -58,8 +58,6 @@
     face_x,
     face_y,
     slots_beside,
-    outgoing,
-    plane_in,
     row_out,
     column_in,
     local_sem,
@@ -68,8 +66,6 @@
     slots_send,
     slots_recv,
     gate,
-    plane_send,
-    plane_recv,
     column_send,
     column_recv,
 ):
@@ -95,20 +91,26 @@
 
     conds, ys, cores, xs, zls = (around(i, n) for i, n in zip((cond, y, core, x, zl), dims))
     steps = [
-        (i, j, k, l)
+        (i, j, c, k, l)
         for i in range(n_cond)
         for j in range(n_y)
+        for c in range(n_core)
         for k in range(n_x)
         for l in range(n_zl)
-        if i or j or k or l
+        if i or j or c or k or l
     ]
-    steps.sort(key=lambda s: -(min(s[1], n_y - s[1]) + min(s[2], n_x - s[2]) + (n_zl if s[0] else s[3])))
-    chip_targets = [
-        ((conds[i], ys[j], core, xs[k], zls[l]), zls[l] * n_y * n_x + ys[j] * n_x + xs[k])
-        for i, j, k, l in steps
+    steps.sort(key=lambda s: -(min(s[1], n_y - s[1]) + min(s[3], n_x - s[3]) + (n_zl if s[0] else s[4])))
+
+    def piece_of(b, c, d, e):
+        return ((e * n_core + c) * n_y + b) * n_x + d
+
+    all_targets = [
+        ((conds[i], ys[j], cores[c], xs[k], zls[l]), piece_of(ys[j], cores[c], xs[k], zls[l]))
+        for i, j, c, k, l in steps
     ]
-    n_chips = len(steps) + 1
-    chip = (cond * n_zl + zl) * n_y * n_x + y * n_x + x
+    n_devices = len(steps) + 1
+    own_piece = piece_of(y, core, x, zl)
+    device = cond * (n_devices // n_cond) + own_piece
 
     barrier = pltpu.get_barrier_semaphore()
 
@@ -407,7 +409,6 @@
 
     open_gate(0, line_gx)
 
-    send_faces(None, 3)
 
     load_source.wait()
 
@@ -416,6 +417,7 @@
         open_gate(1, line_zl)
 
     sweep(start, relaxed, second_gate)
+    send_faces(None, 3)
 
     def weigh(block, carry):
         pull = []
@@ -542,40 +544,26 @@
     whole = jnp.full((n_out, LANES), (weights[0] + weights[1]).astype(jnp.float32))
     mine = jnp.where(cond == 0, weights[0], weights[1]).astype(jnp.float32)
     scaled = (even + swapped) * (jnp.full((n_out, LANES), mine) / whole)
-    outgoing[...] = scaled.reshape(n_out, 1, LANES)
-
-    half = pl.ds(core * half_out, half_out)
-    other = pl.ds((1 - core) * half_out, half_out)
-    pair = pltpu.make_async_remote_copy(
-        src_ref=outgoing.at[other],
-        dst_ref=plane_in,
-        send_sem=plane_send,
-        recv_sem=plane_recv,
-        device_id=(cond, y, 1 - core, x, zl),
-        device_id_type=MESH,
-    )
-    pair.start()
+
+    width = LANES // n_zl
+    for q in range(n_zl):
+        quarter = scaled if q == 0 else pltpu.roll(scaled, LANES - q * width, 1)
+        row_out[pl.ds(q * n_out, n_out)] = quarter[:, :width].reshape(n_out, 1, width)
     pl.semaphore_wait(gate.at[2], 1)
-    pair.wait()
-    width = LANES // n_zl
-    summed = (outgoing[half] + plane_in[...]).reshape(half_out, LANES)
-    for q in range(n_zl):
-        quarter = summed if q == 0 else pltpu.roll(summed, LANES - q * width, 1)
-        row_out[pl.ds(q * half_out, half_out)] = quarter[:, :width].reshape(half_out, 1, width)
-
-    def chip_copy(target, number):
+
+    def piece_copy(target, number):
         return pltpu.make_async_remote_copy(
             src_ref=row_out.at[number],
-            dst_ref=column_in.at[chip],
+            dst_ref=column_in.at[device],
             send_sem=column_send,
             recv_sem=column_recv,
             device_id=target,
             device_id_type=MESH,
         )
 
-    for target, number in chip_targets:
-        chip_copy(target, number).start()
-    column_in[chip] = row_out[zl * n_y * n_x + y * n_x + x]
+    for target, number in all_targets:
+        piece_copy(target, number).start()
+    column_in[device] = row_out[own_piece]
     sweep(relaxed, smoothed)
 
     wait_faces(1)
@@ -593,8 +581,8 @@
     drain_faces(smoothed, 2)
 
     everyone = pltpu.make_async_remote_copy(
-        src_ref=column_in.at[pl.ds(0, n_chips - 1)],
-        dst_ref=column_in.at[pl.ds(0, n_chips - 1)],
+        src_ref=column_in.at[pl.ds(0, n_devices - 1)],
+        dst_ref=column_in.at[pl.ds(0, n_devices - 1)],
         send_sem=column_send,
         recv_sem=column_recv,
         device_id=(cond, y, core, x, zl),
@@ -603,7 +591,7 @@
     everyone.wait_recv()
     groups = 8
     sums = [column_in[i] for i in range(groups)]
-    for i in range(groups, n_chips):
+    for i in range(groups, n_devices):
         sums[i % groups] = sums[i % groups] + column_in[i]
     row = functools.reduce(jnp.add, sums)
     gradient[...] = row
@@ -685,18 +673,14 @@
             pltpu.VMEM((2, nvar, ny * nz // LANES, LANES), f32),
             pltpu.VMEM((4, 2, nvar, nx * nz // LANES, LANES), f32),
             pltpu.VMEM((4, nx, ny), jnp.int32),
-            pltpu.VMEM((NDES // LANES, 1, LANES), f32),
-            pltpu.VMEM((n_y * n_x, 1, LANES), f32),
-            pltpu.VMEM((n_zl * n_y * n_x, 1, LANES // n_zl), f32),
-            pltpu.VMEM((n_cond * n_zl * n_y * n_x, 1, LANES // n_zl), f32),
+            pltpu.VMEM((n_zl * NDES // LANES, 1, LANES // n_zl), f32),
+            pltpu.VMEM((n_cond * n_zl * NDES // LANES, 1, LANES // n_zl), f32),
             dma((9,)),
             dma((4, 4)),
             dma((4, 4)),
             dma((4,)),
             dma((4,)),
             pltpu.SemaphoreType.REGULAR((3,)),
-            dma,
-            dma,
             dma,
             dma,
         ],

time: 27.5 us -> 26.6 us (0.967)
  Pallas kernels: 26.7 us -> 25.9 us
    pallas_call x1, Pallas kernels: 25.7 us -> 24.8 us  [local(): pl.pallas_call(functools.partial(kernel, dims), out_shape=(jax.ShapeDtype...]
where the time goes in v4:
time: 26.6 us; the launch traced here: 26.5 us
  Pallas kernels  25.9 us (97%)
  between operations  0.64 us (2%)
    pallas_call x1, Pallas kernels, local(): pl.pallas_call(functools.partial(kernel, dims), out_shape=(jax.ShapeDtype...  24.8 us
    pallas_call x1, Pallas kernels, local(): pl.pallas_call(put_out, out_shape=tuple((jax.ShapeDtypeStruct(a.shape, a....  1.08 us

profile of v4, /device:TPU:1, one launch (start us, length us, event | category | flops | bytes accessed | tf_op | source)
XLA Modules:
  0.0 26.5 jit_solution(17083760271788716593)
XLA Ops:
  0.6 24.8 %adjoint_step.1 = (f32[5,256,128]{2,1,0:T(8,128)S(1)}, f32[5,256,128]{2,1,0:T(8,128)S(1)}, f32[1,32]{1,0:T(1,128)S(1)}) custom-call(f32[5,256,128]{2,1,0:T(8,128)} %bitcast.33, f32[5,256,128]{2,1,0:T(8,128)} %bitcast.34, f32[256,128]{1,0:T(8,128)} %bitcast.36, bf16[5,128,256]{2,1,0:T(8,128)(2,1)} %bitcast.35, s32[256,128]{1,0:T(8,128)} %bitcast.37, ...), custom_call_target="tpu_custom_call" | custom-call | tf_op jit(solution)/shard_map/adjoint_step/pallas_call | solution.py:644
  25.4 1.1 %put_out.1 = (f32[5,256,128]{2,1,0:T(8,128)}, f32[5,256,128]{2,1,0:T(8,128)}, f32[1,32]{1,0:T(1,128)}) custom-call(f32[5,256,128]{2,1,0:T(8,128)S(1)} %get-tuple-element.9.refs_0_, f32[5,256,128]{2,1,0:T(8,128)S(1)} %get-tuple-element.10.refs_1_, f32[1,32]{1,0:T(1,128)S(1)} %get-tuple-element.11.refs_2_), custom_call_target="tpu_custom_call" | custom-call | tf_op jit(solution)/shard_map/put_out/pallas_call | solution.py:708

commit v5 on v4

--- a/solution.py
+++ b/solution.py
@@ -207,13 +207,14 @@
 
     far = (zl == 0, zl == n_zl - 1)
 
-    def send_faces(field, turn):
+    def send_far(field, turn):
         for side in range(2):
 
             @pl.when(jnp.logical_and(sides[1][side], far[side]))
             def _(side=side):
                 halo_copy(field, turn, 1, side).start()
 
+    def send_near(field, turn):
         for side in range(2):
 
             @pl.when(jnp.logical_not(far[side]))
@@ -225,6 +226,10 @@
             @pl.when(sides[0][side])
             def _(side=side):
                 halo_copy(field, turn, 0, side).start()
+
+    def send_faces(field, turn):
+        send_far(field, turn)
+        send_near(field, turn)
 
     def slots_copy(axis, side):
         index = 2 * axis + side
@@ -399,7 +404,7 @@
     pl.semaphore_wait(
         barrier, len(greeted) + step_up.astype(jnp.int32) + step_down.astype(jnp.int32)
     )
-    send_faces(start, 0)
+    send_far(start, 0)
     each_side(lambda axis, side: slots_copy(axis, side).start())
     line_zl = [(cond, y, core, x, e) for e in zls[1:]]
 
@@ -413,11 +418,13 @@
     load_source.wait()
 
     def second_gate():
+        send_far(None, 3)
+        send_near(None, 3)
         pl.semaphore_wait(gate.at[0], len(line_gx))
         open_gate(1, line_zl)
 
+    send_near(start, 0)
     sweep(start, relaxed, second_gate)
-    send_faces(None, 3)
 
     def weigh(block, carry):
         pull = []
@@ -589,11 +596,7 @@
         device_id_type=MESH,
     )
     everyone.wait_recv()
-    groups = 8
-    sums = [column_in[i] for i in range(groups)]
-    for i in range(groups, n_devices):
-        sums[i % groups] = sums[i % groups] + column_in[i]
-    row = functools.reduce(jnp.add, sums)
+    row = jnp.sum(column_in[...].reshape(n_devices, LANES // n_zl), axis=0, keepdims=True)
     gradient[...] = row
     everyone.wait_send()
 

time: 26.6 us -> 26.5 us (level)
  no operation moved by 1% of the time
where the time goes in v5:
time: 26.5 us; the launch traced here: 26.4 us
  Pallas kernels  25.8 us (97%)
  between operations  0.64 us (2%)
    pallas_call x1, Pallas kernels, local(): pl.pallas_call(functools.partial(kernel, dims), out_shape=(jax.ShapeDtype...  24.7 us
    pallas_call x1, Pallas kernels, local(): pl.pallas_call(put_out, out_shape=tuple((jax.ShapeDtypeStruct(a.shape, a....  1.08 us

profile of v5, /device:TPU:1, one launch (start us, length us, event | category | flops | bytes accessed | tf_op | source)
XLA Modules:
  0.0 26.4 jit_solution(5592600712671304148)
XLA Ops:
  0.6 24.7 %adjoint_step.1 = (f32[5,256,128]{2,1,0:T(8,128)S(1)}, f32[5,256,128]{2,1,0:T(8,128)S(1)}, f32[1,32]{1,0:T(1,128)S(1)}) custom-call(f32[5,256,128]{2,1,0:T(8,128)} %bitcast.33, f32[5,256,128]{2,1,0:T(8,128)} %bitcast.34, f32[256,128]{1,0:T(8,128)} %bitcast.36, bf16[5,128,256]{2,1,0:T(8,128)(2,1)} %bitcast.35, s32[256,128]{1,0:T(8,128)} %bitcast.37, ...), custom_call_target="tpu_custom_call" | custom-call | tf_op jit(solution)/shard_map/adjoint_step/pallas_call | solution.py:647
  25.3 1.1 %put_out.1 = (f32[5,256,128]{2,1,0:T(8,128)}, f32[5,256,128]{2,1,0:T(8,128)}, f32[1,32]{1,0:T(1,128)}) custom-call(f32[5,256,128]{2,1,0:T(8,128)S(1)} %get-tuple-element.9.refs_0_, f32[5,256,128]{2,1,0:T(8,128)S(1)} %get-tuple-element.10.refs_1_, f32[1,32]{1,0:T(1,128)S(1)} %get-tuple-element.11.refs_2_), custom_call_target="tpu_custom_call" | custom-call | tf_op jit(solution)/shard_map/put_out/pallas_call | solution.py:711
